TPU v7x, 128 devices: a whole 4x4x4 slice. The times are simulated.
128 devices in a mesh: dp: 16 (over x_hi, z, core), mp: 8 (over y, x_lo).
Axes of the slice: x: 4 (x_hi: 2, x_lo: 2; x = x_hi * 2 + x_lo), y: 4, z: 4, core: 2. Of those that a mesh axis runs over, the one named last changes fastest.
Arguments:
- events: bfloat16 [4096, 128, 8, 128], P('dp', 'mp'), may hold values from -32 to 32
- lengths: int32 [4096, 128], P('dp', 'mp'), may hold values from 2 to 8, as said below
- query_vecs: bfloat16 [128, 128], P('mp'), may hold values from -5 to 5
- fm_proj: bfloat16 [128, 8], replicated, may hold values from -0.5 to 0.5
- up_weight: bfloat16 [1024, 16384], P(None, 'mp'), may hold values from -0.1875 to 0.1875
- down_weight: bfloat16 [16384, 512], P('mp'), may hold values from -0.046875 to 0.046875
- cotangent: bfloat16 [4096, 512], P('dp', 'mp'), may hold values from -1.5 to 1.5
Outputs:
- block_out: bfloat16 [4096, 512], P('dp', 'mp')
- grad_up: float32 [1024, 16384], P(None, 'mp')
- grad_down: float32 [16384, 512], P('mp')
- grad_pooled: bfloat16 [4096, 128, 128], P('dp', 'mp')
- grad_query: float32 [128, 128], P('mp')
Inputs may be any that keep to these rules, and one draw needn't show every extreme that they name: `lengths`: every length of the first user equals 8.
All inputs are finite; a program needn't handle non-finite values.
Results may differ from a plain program's by a relative error of at most 0.024.
Values may be sent and summed in bfloat16 or wider, within the bound.
No kernel may reach another device: no remote copies, remote signals or barrier semaphores. Data moves between devices by JAX's collectives and lax.ppermute only.
A program may use at most 128 MiB of HBM per device.

v0:
```python
import math

import jax
import jax.numpy as jnp
from jax import lax
from jax.sharding import PartitionSpec as P

norm_eps = 1e-05
highest = lax.Precision.HIGHEST


def per_device(events, lengths, query_vecs, fm_proj, up_weight, down_weight, cotangent):
    users_here, feats_here, seq_len, emb_width = events.shape
    all_feats, rank_width = fm_proj.shape
    score_scale = 1.0 / math.sqrt(emb_width)
    scores = (
        jnp.einsum("bfle,fe->bfl", events, query_vecs, preferred_element_type=jnp.float32)
        * score_scale
    )
    positions = lax.broadcasted_iota(jnp.int32, scores.shape, 2)
    live_mask = positions < lengths[:, :, None]
    row_top = jnp.max(jnp.where(live_mask, scores, -1e30), axis=-1, keepdims=True)
    exp_scores = jnp.exp(jnp.where(live_mask, scores - row_top, -1e30))
    weights = exp_scores / jnp.sum(exp_scores, axis=-1, keepdims=True)
    pooled = jnp.einsum(
        "bfl,bfle->bfe", weights.astype(jnp.bfloat16), events, preferred_element_type=jnp.float32
    ).astype(jnp.bfloat16)
    first_feat = lax.axis_index("mp") * feats_here
    proj_here = lax.dynamic_slice_in_dim(fm_proj, first_feat, feats_here, 0)
    all_pooled = lax.all_gather(pooled, "mp", axis=1, tiled=True)
    proj_mix = jnp.einsum(
        "bfe,fr->bre", all_pooled, fm_proj, preferred_element_type=jnp.float32
    ).astype(jnp.bfloat16)
    fm_full = jnp.einsum(
        "bfe,bre->bfr", all_pooled, proj_mix, preferred_element_type=jnp.float32
    ).reshape(users_here, -1)
    inv_rms = lax.rsqrt(jnp.mean(fm_full * fm_full, axis=-1, keepdims=True) + norm_eps)
    normed = fm_full * inv_rms
    normed_rows = normed.astype(jnp.bfloat16)
    hidden = jnp.dot(normed_rows, up_weight, preferred_element_type=jnp.float32)
    activated = jax.nn.silu(hidden).astype(jnp.bfloat16)
    out_terms = jnp.dot(activated, down_weight, preferred_element_type=jnp.float32)
    block_out = lax.psum_scatter(
        out_terms.astype(jnp.bfloat16), "mp", scatter_dimension=1, tiled=True
    )
    cot_full = lax.all_gather(cotangent, "mp", axis=1, tiled=True)
    part_down = lax.dot_general(
        activated, cot_full, (((0,), (0,)), ((), ())), preferred_element_type=jnp.float32
    )
    d_act = lax.dot_general(
        cot_full, down_weight, (((1,), (1,)), ((), ())), preferred_element_type=jnp.float32
    )
    sig_hidden = jax.nn.sigmoid(hidden)
    d_hidden = (d_act * sig_hidden * (1.0 + hidden * (1.0 - sig_hidden))).astype(jnp.bfloat16)
    part_up = lax.dot_general(
        normed_rows, d_hidden, (((0,), (0,)), ((), ())), preferred_element_type=jnp.float32
    )
    d_normed = lax.dot_general(
        d_hidden, up_weight, (((1,), (1,)), ((), ())), preferred_element_type=jnp.float32
    )
    d_normed = lax.psum(d_normed.astype(jnp.bfloat16), "mp").astype(jnp.float32)
    grad_fm = inv_rms * (d_normed - normed * jnp.mean(d_normed * normed, axis=-1, keepdims=True))
    grad_cube = grad_fm.reshape(users_here, all_feats, rank_width)
    grad_here = lax.dynamic_slice_in_dim(grad_cube, first_feat, feats_here, 1)
    back_proj = jnp.einsum(
        "bfe,bfr->bre", all_pooled.astype(jnp.float32), grad_cube, precision=highest
    )
    pooled_grad = jnp.einsum(
        "bfr,bre->bfe", grad_here, proj_mix.astype(jnp.float32), precision=highest
    )
    pooled_grad = pooled_grad + jnp.einsum(
        "fr,bre->bfe", proj_here.astype(jnp.float32), back_proj, precision=highest
    )
    grad_pooled = pooled_grad.astype(jnp.bfloat16)
    contrib = jnp.einsum("bfle,bfe->bfl", events, grad_pooled, preferred_element_type=jnp.float32)
    d_scores = (weights * (contrib - jnp.sum(weights * contrib, axis=-1, keepdims=True))).astype(
        jnp.bfloat16
    )
    query_term = (
        jnp.einsum("bfl,bfle->fe", d_scores, events, preferred_element_type=jnp.float32)
        * score_scale
    )
    grad_up, grad_down, grad_query = (
        lax.psum(part_up.astype(jnp.bfloat16), "dp").astype(jnp.float32),
        lax.psum(part_down.astype(jnp.bfloat16), "dp").astype(jnp.float32),
        lax.psum(query_term.astype(jnp.bfloat16), "dp").astype(jnp.float32),
    )
    return (block_out, grad_up, grad_down, grad_pooled, grad_query)


def solution(mesh):
    in_specs = (
        P("dp", "mp", None, None),
        P("dp", "mp"),
        P("mp", None),
        P(),
        P(None, "mp"),
        P("mp", None),
        P("dp", "mp"),
    )
    out_specs = (P("dp", "mp"), P(None, "mp"), P("mp", None), P("dp", "mp", None), P("mp", None))
    return jax.shard_map(
        per_device, mesh=mesh, in_specs=in_specs, out_specs=out_specs, check_vma=False
    )
```

profile of v0, /device:TPU:0, one launch (start us, length us, event | category | flops | bytes accessed | tf_op | source)
XLA Modules:
  0.0 549.6 jit_solution(876030209921210141)
XLA Ops:
  7.2 0.0 copy-start
  7.2 0.0 all-gather.2.cloned.1.call-start
  7.2 42.0 %fusion.5 = f32[16,1,256,8]{3,1,2,0:T(1,128)} fusion(bf16[256,16,8,128]{3,2,1,0:T(8,128)(2,1)} %param.7, bf16[16,128,1,1]{1,0,2,3:T(8,128)(2,1)} %bitcast.74), kind=kOutput, calls=%fused_computation.5 | convolution fusion | flops 8388608 | bytes 8523776 | tf_op jit(solution)/shard_map/bfle,fe->bfl/dot_general | solution.py:17
  49.2 4.4 copy.26
  53.6 0.0 copy-done.14
  53.6 0.1 fusion.12
  53.7 3.7 copy.27
  57.4 7.2 %fusion.41 = f32[256,16,1,128]{3,2,1,0:T(1,128)S(1)} fusion(bf16[256,16,8,1]{2,3,1,0:T(2,128)(2,1)} %copy.27, bf16[256,16,8,128]{3,2,1,0:T(8,128)(2,1)} %param.7), kind=kOutput, calls=%fused_computation.60 | convolution fusion | flops 8388608 | bytes 10551296 | tf_op jit(solution)/shard_map/bfl,bfle->bfe/dot_general | solution.py:25
  64.6 0.0 copy-start.12
  64.6 0.0 copy-start.13
  64.6 1.1 convert_element_type.56
  65.7 0.0 all-gather.2.cloned.1.call-update
  65.8 0.0 all-reduce.4.cloned.1.call-start
  65.8 0.0 copy-done.12
  65.8 44.1 %all_gather.7 = bf16[256,512]{0,1:T(8,128)(2,1)} all-gather(bf16[256,64]{0,1:T(8,128)(2,1)S(1)} %copy-done.12), channel_id=1, replica_groups=mesh['dp'=16,'mp'=8] {'mp'}, dimensions={1}, use_global_device_ids=true | all-gather | bytes 294912 | tf_op jit(solution)/shard_map/all_gather | solution.py:46
  109.9 131.4 %all-gather.2.cloned.1.call-done = bf16[256,128,128]{2,1,0:T(8,128)(2,1)} async-done(((bf16[256,16,128]{2,1,0:T(8,128)(2,1)}), bf16[256,128,128]{2,1,0:T(8,128)(2,1)}) %all-gather.2.cloned.1.call-update) | async-done | bytes 8388624 | tf_op jit(solution)/shard_map/all_gather | solution.py:30
  241.3 0.0 copy-done.13
  241.4 4.7 convolution_convert_fusion.2
  246.1 1.1 copy-done.2
  247.1 4.8 multiply_reduce_fusion
  251.9 0.0 copy-done.3
  251.9 1.5 copy.19
  253.4 1.6 copy.20
  255.0 0.0 copy-start.10
  255.0 3.5 fusion.38
  258.5 0.0 copy-start.6
  258.5 1.3 copy-done.6
  259.8 0.0 copy-done
  259.8 1.1 fusion.8
  260.9 0.0 copy-start.8
  260.9 1.0 copy-done.8
  261.9 0.5 copy-done.4
  262.4 2.1 convolution_convert_fusion.3
  264.5 0.0 all-reduce.4.cloned.1.call-update
  264.5 0.0 all-reduce.6.cloned.1.call-start
  264.5 0.0 copy-start.7
  264.6 4.8 convolution_convert_fusion
  269.3 0.0 copy-done.11
  269.3 2.2 convolution_convert_fusion.1
  271.6 0.0 all-reduce.6.cloned.1.call-update
  271.6 0.0 reduce-scatter.2.cloned.1.call-start
  271.6 3.4 convolution_convert_fusion.4
  275.1 0.0 reduce-scatter.2.cloned.1.call-update
  275.1 66.6 %all-reduce.4.cloned.1.call-done = bf16[256,1024]{1,0:T(8,128)(2,1)} async-done(((bf16[256,1024]{1,0:T(8,128)(2,1)}), bf16[256,1024]{1,0:T(8,128)(2,1)}) %all-reduce.4.cloned.1.call-update) | async-done | bytes 524304 | tf_op jit(solution)/shard_map/psum | solution.py:61
  341.7 1.3 fusion.20
  343.0 1.3 fusion.21
  344.3 0.3 copy.21
  344.7 0.6 copy.22
  345.2 3.2 fusion.22
  348.4 9.1 %fusion.42 = f32[256,8,128]{2,1,0:T(8,128)S(1)} fusion(f32[256,128,8]{1,2,0:T(8,128)S(1)} %copy.22, bf16[256,128,128]{2,1,0:T(8,128)(2,1)} %all-gather.2.cloned.1.call-done), kind=kOutput, calls=%fused_computation.61 | convolution fusion | flops 402653184 | bytes 10485760 | tf_op jit(solution)/shard_map/bfe,bfr->bre/dot_general | solution.py:65
  357.6 1.2 fusion.9
  358.7 0.0 copy-start.9
  358.8 8.4 %fusion.10 = f32[256,16,1,8]{3,2,1,0:T(1,128)S(1)} fusion(bf16[256,16,8,128]{3,2,1,0:T(8,128)(2,1)} %param.7, bf16[256,16,128,1]{2,1,0,3:T(8,128)(2,1)S(1)} %bitcast.73), kind=kOutput, calls=%fused_computation.16 | convolution fusion | flops 8388608 | bytes 9568256 | tf_op jit(solution)/shard_map/bfle,bfe->bfl/dot_general | solution.py:75
  367.2 1.6 copy.30
  368.7 0.1 fusion.19
  368.8 1.4 copy.31
  370.2 8.2 %fusion.3 = f32[16,1,128,1]{2,1,3,0:T(1,128)S(1)} fusion(bf16[256,16,8,1]{2,3,0,1:T(2,128)(2,1)S(1)} %copy.31, bf16[256,16,8,128]{3,2,1,0:T(8,128)(2,1)} %param.7), kind=kOutput, calls=%fused_computation.3 | convolution fusion | flops 8388608 | bytes 8462336 | tf_op jit(solution)/shard_map/bfl,bfle->fe/dot_general | solution.py:80
  378.4 33.2 %psum.31 = bf16[16,128]{1,0:T(8,128)(2,1)S(1)} all-reduce(bf16[16,128]{1,0:T(8,128)(2,1)S(1)} %multiply_convert_fusion.2), channel_id=1, replica_groups=mesh['dp'=16,'mp'=8] {'dp'}, use_global_device_ids=true, to_apply=%region_9.10 | all-reduce | flops 2048 | bytes 8192 | tf_op jit(solution)/shard_map/psum | solution.py:86
  411.6 0.6 convert_element_type.71
  412.2 89.5 %all-reduce.6.cloned.1.call-done = (bf16[1024,2048]{1,0:T(8,128)(2,1)}, bf16[2048,512]{1,0:T(8,128)(2,1)}) async-done(((bf16[1024,2048]{1,0:T(8,128)(2,1)}, bf16[2048,512]{1,0:T(8,128)(2,1)}), (bf16[1024,2048]{1,0:T(8,128)(2,1)}, bf16[2048,512]{1,0:T(8,128)(2,1)})) %all-reduce.6.cloned.1.call-update) | async-done | bytes 6291472 | tf_op jit(solution)/shard_map/psum | solution.py:84
  501.6 6.8 %convert_element_type.63 = f32[1024,2048]{1,0:T(8,128)} convert(bf16[1024,2048]{1,0:T(8,128)(2,1)} %get-tuple-element.5) | non-fusion elementwise | flops 2097152 | bytes 12582912 | tf_op jit(solution)/shard_map/convert_element_type | solution.py:84
  508.4 0.0 copy-done.5
  508.4 2.6 convert_element_type.65
  511.1 31.6 %reduce-scatter.2.cloned.1.call-done = bf16[256,64]{0,1:T(8,128)(2,1)} async-done(((bf16[256,512]{0,1:T(8,128)(2,1)}), bf16[256,64]{0,1:T(8,128)(2,1)}) %reduce-scatter.2.cloned.1.call-update) | async-done | bytes 32784 | tf_op jit(solution)/shard_map/reduce_scatter | solution.py:43
  (15 shorter events, 0.0 us)
Async XLA Ops:
  7.2 252.7 %copy-start = (bf16[2048,512]{1,0:T(8,128)(2,1)S(1)}, bf16[2048,512]{1,0:T(8,128)(2,1)}, u32[]{:S(2)}) copy-start(bf16[2048,512]{1,0:T(8,128)(2,1)} %param.12) | copy-start | bytes 6291460
  7.2 234.2 %all-gather.2.cloned.1.call-start = ((), (), s32[]{:S(2)}) async-start(), calls=%async_computation.1 | async-start | bytes 9437184 | tf_op jit(solution)/shard_map/all_gather | solution.py:30
  49.2 4.4 copy-start.14
  64.6 1.2 copy-start.12
  64.6 176.7 %copy-start.13 = (bf16[128,8]{0,1:T(8,128)(2,1)S(1)}, bf16[128,8]{0,1:T(8,128)(2,1)}, u32[]{:S(2)}) copy-start(bf16[128,8]{0,1:T(8,128)(2,1)} %param.10) | copy-start | bytes 6148
  65.8 275.9 %all-reduce.4.cloned.1.call-start = ((), (), s32[]{:S(2)}) async-start(), calls=%async_computation.3 | async-start | bytes 1048576 | tf_op jit(solution)/shard_map/psum | solution.py:61
  241.3 5.8 %copy-start.2 = (bf16[256,128,128]{2,1,0:T(8,128)(2,1)S(1)}, bf16[256,128,128]{2,1,0:T(8,128)(2,1)}, u32[]{:S(2)}) copy-start(bf16[256,128,128]{2,1,0:T(8,128)(2,1)} %all-gather.2.cloned.1.call-done) | copy-start | bytes 25165828
  247.1 4.8 copy-start.3
  255.0 4.9 copy-start.10
  258.5 1.3 copy-start.6
  259.8 2.5 copy-start.4
  260.9 1.0 copy-start.8
  264.5 237.1 %all-reduce.6.cloned.1.call-start = ((), (), s32[]{:S(2)}) async-start(), calls=%async_computation.4 | async-start | bytes 12582912 | tf_op jit(solution)/shard_map/psum | solution.py:84
  264.5 4.8 copy-start.7
  264.6 4.8 copy-start.11
  271.6 271.1 %reduce-scatter.2.cloned.1.call-start = ((), (), s32[]{:S(2)}) async-start(), calls=%async_computation.2 | async-start | bytes 294912 | tf_op jit(solution)/shard_map/reduce_scatter | solution.py:43
  358.7 8.4 %copy-start.9 = (bf16[256,16,128]{2,1,0:T(8,128)(2,1)}, bf16[256,16,128]{2,1,0:T(8,128)(2,1)S(1)}, u32[]{:S(2)}) copy-start(bf16[256,16,128]{2,1,0:T(8,128)(2,1)S(1)} %fusion.9) | copy-start | bytes 3145732
  501.6 6.8 %copy-start.5 = (bf16[2048,512]{1,0:T(8,128)(2,1)S(1)}, bf16[2048,512]{1,0:T(8,128)(2,1)}, u32[]{:S(2)}) copy-start(bf16[2048,512]{1,0:T(8,128)(2,1)} %get-tuple-element.6) | copy-start | bytes 6291460
  508.4 34.2 %copy-start.1 = (bf16[2048,512]{1,0:T(8,128)(2,1)S(1)}, bf16[2048,512]{1,0:T(8,128)(2,1)}, u32[]{:S(2)}) copy-start(bf16[2048,512]{1,0:T(8,128)(2,1)} %param.12) | copy-start | bytes 6291460
Sparse Core Ops, SparseCore 0:
  65.9 175.4 all-gather.1
  264.6 77.0 all-reduce.3
  344.9 156.7 all-reduce.5
  504.4 38.2 reduce-scatter.1
where the time goes:
time: 559 us; the launch traced here: 550 us
  waiting for transfers between devices  319 us (57%)
  matrix products  106 us (19%)
  blocking collectives  77.3 us (14%)
  local copies, waits for them, and re-layouts  18.9 us (3%)
  between operations  14.4 us (3%)
  other arithmetic  13.9 us (2%)
    all_gather x1, waiting for transfers between devices, per_device(): all_pooled = lax.all_gather(pooled, 'mp', axis=1, tiled=True)  131 us
    psum x1, waiting for transfers between devices, per_device(): lax.psum(part_up.astype(jnp.bfloat16), 'dp').astype(jnp.float32)  89.5 us
    psum x1, waiting for transfers between devices, per_device(): d_normed = lax.psum(d_normed.astype(jnp.bfloat16), 'mp').astype(jnp.float32)  66.6 us
    all_gather x1, blocking collectives, per_device(): cot_full = lax.all_gather(cotangent, 'mp', axis=1, tiled=True)  44.1 us
    dot_general x1, matrix products, per_device(): jnp.einsum('bfle,fe->bfl', events, query_vecs, preferred_element_type=jnp...  42 us
    psum x1, blocking collectives, per_device(): lax.psum(query_term.astype(jnp.bfloat16), 'dp').astype(jnp.float32)  33.2 us
    reduce_scatter x1, waiting for transfers between devices, per_device(): lax.psum_scatter(out_terms.astype(jnp.bfloat16), 'mp', scatter_dimension=...  31.6 us
  transfers between devices with their start and end apart: 4, of which 4 were waited for; matrix products, arithmetic and copies ran while one was open for 10% of the time, Pallas kernels for 0%

commit v1 on v0

v1 whole, which is shorter than its diff:
```python
import math

import jax
import jax.numpy as jnp
from jax import lax
from jax.experimental import pallas as pl
from jax.experimental.pallas import tpu as pltpu
from jax.sharding import PartitionSpec as P


norm_eps = 1e-05
f32 = jnp.float32
bf16 = jnp.bfloat16


E = 128
L = 8
R = 8
MP = 8
FH = 16
UB = 32
U = 256
NT = (((1,), (1,)), ((), ()))
TN = (((0,), (0,)), ((), ()))
NN = (((1,), (0,)), ((), ()))


def dot(a, b, dims=NN):
    return lax.dot_general(a, b, dims, preferred_element_type=f32)


def iota(shape, axis):
    return lax.broadcasted_iota(jnp.int32, shape, axis)


def own_lanes():
    return iota((FH, E), 0) == iota((FH, E), 1) // L


def group_reduce(x, op):
    lane = iota(x.shape, 1)
    for s in (1, 2, 4):
        up = pltpu.roll(x, E - s, 1)
        down = pltpu.roll(x, s, 1)
        x = op(x, jnp.where((lane & s) == 0, up, down))
    return x


def pool_kernel(ev_ref, len_ref, q_ref, cot_ref, send_ref, w_ref, scr):
    mask = own_lanes()
    raw = dot(q_ref[...], ev_ref[...], NT)
    for u in range(UB):
        block = jnp.where(mask, raw[:, u * E : (u + 1) * E], 0.0)
        scr[u : u + 1, :] = jnp.sum(block, axis=0, keepdims=True)
    scores = scr[...] * (1.0 / math.sqrt(E))
    spread = mask.astype(f32).astype(bf16)
    lens = dot(len_ref[...].astype(f32).astype(bf16), spread)
    live = (iota((UB, E), 1) % L).astype(f32) < lens
    top = group_reduce(jnp.where(live, scores, -1e30), jnp.maximum)
    ex = jnp.exp(jnp.where(live, scores - top, -1e30))
    w = ex / group_reduce(ex, jnp.add)
    w_ref[...] = w
    scr[...] = w
    for u in range(UB):
        row = jnp.broadcast_to(scr[u : u + 1, :], (FH, E))
        mix = jnp.where(mask, row, 0.0).astype(bf16)
        pooled = dot(mix, ev_ref[u * E : (u + 1) * E, :])
        send_ref[0, u * FH : (u + 1) * FH, :] = pooled.astype(bf16)
    send_ref[0, UB * FH :, 0:64] = cot_ref[0 : U // 2, :]
    send_ref[0, UB * FH :, 64:128] = cot_ref[U // 2 :, :]


def pool_call(ev, lens, q, cot):
    rows = UB * FH + U // 2
    return pl.pallas_call(
        pool_kernel,
        grid=(MP,),
        in_specs=[
            pl.BlockSpec((UB * E, E), lambda i: (i, 0)),
            pl.BlockSpec((UB, FH), lambda i: (i, 0)),
            pl.BlockSpec((FH, E), lambda i: (0, 0)),
            pl.BlockSpec((U, 64), lambda i: (0, 0)),
        ],
        out_specs=[
            pl.BlockSpec((1, rows, E), lambda i: (i, 0, 0)),
            pl.BlockSpec((UB, E), lambda i: (i, 0)),
        ],
        out_shape=[
            jax.ShapeDtypeStruct((MP, rows, E), bf16),
            jax.ShapeDtypeStruct((U, E), f32),
        ],
        scratch_shapes=[pltpu.VMEM((UB, E), f32)],
        name="pool",
    )(ev, lens, q, cot)


def flat_mask():
    return iota((E, E), 0) % FH == iota((E, E), 1) // R


def tile_ranks(m):
    pair = jnp.concatenate([m, m], axis=0).astype(bf16)
    return jnp.concatenate([pair] * 8, axis=0)


def user_rows(ref, u):
    return jnp.concatenate(
        [ref[j, pl.ds(pl.multiple_of(u * FH, FH), FH), :] for j in range(MP)], axis=0
    )


def fm_kernel(recv_ref, projt_ref, send_ref, normed_ref, inv_ref, mix_ref, cot_ref, scr):
    mask = flat_mask()
    projt = projt_ref[...]

    def step(u, carry):
        p = user_rows(recv_ref, u)
        mix = dot(projt, p)[0:R].astype(bf16).astype(f32)
        full = jnp.where(mask, dot(p, tile_ranks(mix), NT), 0.0)
        at = pl.multiple_of(u * R, R)
        mix_ref[pl.ds(at, R), :] = mix
        scr[pl.ds(at, R), :] = jnp.sum(full.reshape(MP, FH, E), axis=1)
        return carry

    lax.fori_loop(0, UB, step, 0, unroll=8)
    total = jnp.zeros((UB, 1), f32)
    for j in range(MP):
        x = scr[pl.ds(j, UB, stride=R), :]
        total = total + jnp.sum(x * x, axis=1, keepdims=True)
    inv = lax.rsqrt(total * (1.0 / (E * R)) + norm_eps)
    inv_ref[...] = jnp.broadcast_to(inv, (UB, E))
    for j in range(MP):
        x = scr[pl.ds(j, UB, stride=R), :] * inv
        normed_ref[:, j * E : (j + 1) * E] = x
        for p in range(MP):
            send_ref[p, :, j * E : (j + 1) * E] = x.astype(bf16)
    at = UB * FH
    half = U // 2
    for j in range(MP):
        cot_ref[0:half, j * 64 : (j + 1) * 64] = recv_ref[j, at:, 0:64]
        cot_ref[half:, j * 64 : (j + 1) * 64] = recv_ref[j, at:, 64:128]


def fm_call(recv, projt):
    return pl.pallas_call(
        fm_kernel,
        out_shape=[
            jax.ShapeDtypeStruct((MP, UB, E * R), bf16),
            jax.ShapeDtypeStruct((UB, E * R), f32),
            jax.ShapeDtypeStruct((UB, E), f32),
            jax.ShapeDtypeStruct((UB * R, E), f32),
            jax.ShapeDtypeStruct((U, 512), bf16),
        ],
        scratch_shapes=[pltpu.VMEM((UB * R, E), f32)],
        name="fm_forward",
    )(recv, projt)


HB = 256
STEPS = 4


def layer_step(i, n_ref, cot_ref, up_ref, down_ref, g_ref, out_acc, dn_acc):
    n = n_ref[...]
    cot = cot_ref[...]
    up = up_ref[...]
    down = down_ref[...]
    hidden = dot(n, up)
    d_act = dot(cot, down, NT)
    s = 1.0 / (1.0 + jnp.exp(-hidden))
    act = (hidden * s).astype(bf16)
    d_hidden = (d_act * s * (1.0 + hidden * (1.0 - s))).astype(bf16)
    out_acc[...] += dot(act, down)
    dn_acc[...] += dot(d_hidden, up, NT)
    g_up = dot(n, d_hidden, TN).astype(bf16).reshape(MP, E, HB)
    g_down = dot(act, cot, TN).astype(bf16)
    for k in range(STEPS):

        @pl.when(i == k)
        def _():
            g_ref[:, 0:E, k * HB : (k + 1) * HB] = g_up
            for t in range(2):
                for h in range(2):
                    at = t * 128 + h * 64
                    g_ref[2 * k + t, E : E + 64, h * 512 : (h + 1) * 512] = g_down[at : at + 64, :]


def layer_first(base_ref, rank_ref, n_ref, cot_ref, up_ref, down_ref, g_ref, out_ref, dn_ref):
    i = pl.program_id(0)

    @pl.when(i == 0)
    def _():
        out_ref[...] = jnp.zeros_like(out_ref)
        dn_ref[...] = jnp.zeros_like(dn_ref)

    layer_step(i, n_ref, cot_ref, up_ref, down_ref, g_ref, out_ref, dn_ref)


def layer_second(
    base_ref, rank_ref, n_ref, cot_ref, up_ref, down_ref, out_in, dn_in, g_ref, *refs
):
    sends, (out_acc, dn_acc, packed) = refs[:MP], refs[MP:]
    i = pl.program_id(0)

    @pl.when(i == 0)
    def _():
        out_acc[...] = out_in[...]
        dn_acc[...] = dn_in[...]

    layer_step(i, n_ref, cot_ref, up_ref, down_ref, g_ref, out_acc, dn_acc)

    @pl.when(i == STEPS - 1)
    def _():
        for p in range(MP):
            for g in range(16):
                packed[p, :, g * 64 : (g + 1) * 64] = out_acc[
                    g * 16 : (g + 1) * 16, p * 64 : (p + 1) * 64
                ].astype(bf16)
        for s in range(MP):
            p = rank_ref[0] ^ s
            sends[s][0:UB, :] = dn_acc[pl.ds(pl.multiple_of(p * UB, UB), UB), :].astype(bf16)
            sends[s][UB : UB + 16, :] = packed[p]


def layer_call(base, rank, n, cot, up, down, partial=None):
    whole = lambda shape: pl.BlockSpec(shape, lambda i, b, r: (0,) * len(shape))
    in_specs = [
        whole((U, E * R)),
        whole((U, 512)),
        pl.BlockSpec((E * R, HB), lambda i, b, r: (0, b[0] + i)),
        pl.BlockSpec((HB, 512), lambda i, b, r: (b[0] + i, 0)),
    ]
    args = [n, cot, up, down]
    g_spec, g_shape = whole((MP, 192, 1024)), jax.ShapeDtypeStruct((MP, 192, 1024), bf16)
    acc_shapes = [(U, 512), (U, E * R)]
    if partial is None:
        body, scratch = layer_first, []
        out_specs = [g_spec] + [whole(s) for s in acc_shapes]
        out_shape = [g_shape] + [jax.ShapeDtypeStruct(s, f32) for s in acc_shapes]
    else:
        body, scratch = layer_second, [pltpu.VMEM(s, f32) for s in acc_shapes]
        scratch.append(pltpu.VMEM((MP, 16, 1024), bf16))
        in_specs += [whole(s) for s in acc_shapes]
        args += list(partial)
        out_specs = [g_spec] + [whole((48, 1024))] * MP
        out_shape = [g_shape] + [jax.ShapeDtypeStruct((48, 1024), bf16)] * MP
    return pl.pallas_call(
        body,
        grid_spec=pltpu.PrefetchScalarGridSpec(
            num_scalar_prefetch=2,
            grid=(STEPS,),
            in_specs=in_specs,
            out_specs=out_specs,
            scratch_shapes=scratch,
        ),
        out_shape=out_shape,
        name="layer_first" if partial is None else "layer_second",
    )(base, rank, *args)


def fm_back_kernel(rank_ref, *refs):
    dns = refs[:MP]
    recv_ref, projpad_ref, normed_ref, inv_ref, mix_ref = refs[MP : MP + 5]
    sends = refs[MP + 5 : 2 * MP + 5]
    block_ref, scr, rows = refs[2 * MP + 5 :]
    mask = flat_mask()
    inv = inv_ref[...][:, 0:1]
    dots = jnp.zeros((UB, 1), f32)
    for j in range(MP):
        at = slice(j * E, (j + 1) * E)
        d = dns[0][0:UB, at].astype(f32)
        for s in range(1, MP):
            d = d + dns[s][0:UB, at].astype(f32)
        scr[pl.ds(j, UB, stride=R), :] = d
        dots = dots + jnp.sum(d * normed_ref[:, at], axis=1, keepdims=True)
    mean = dots * (1.0 / (E * R))
    for j in range(MP):
        at = slice(j * E, (j + 1) * E)
        d = scr[pl.ds(j, UB, stride=R), :]
        scr[pl.ds(j, UB, stride=R), :] = inv * (d - normed_ref[:, at] * mean)
    projpad = projpad_ref[...]

    def step(u, carry):
        at = pl.multiple_of(u * R, R)
        p = user_rows(recv_ref, u)
        g = scr[pl.ds(at, R), :]
        spread = jnp.concatenate(
            [jnp.broadcast_to(g[j : j + 1, :], (FH, E)) for j in range(MP)], axis=0
        )
        spread = jnp.where(mask, spread, 0.0).astype(bf16)
        back = jnp.sum(dot(spread, p, TN).reshape(FH, R, E), axis=0)
        high = back.astype(bf16).astype(f32)
        pair = jnp.concatenate([high, back - high], axis=0).astype(bf16)
        back_rows = jnp.concatenate([pair] * 8, axis=0)
        left = jnp.concatenate([spread, projpad], axis=1)
        right = jnp.concatenate([tile_ranks(mix_ref[pl.ds(at, R), :]), back_rows], axis=0)
        grad = dot(left, right).astype(bf16)
        for j in range(MP):
            rows[j, pl.ds(pl.multiple_of(u * FH, FH), FH), :] = grad[j * FH : (j + 1) * FH, :]
        return carry

    lax.fori_loop(0, UB, step, 0, unroll=8)
    for s in range(MP):
        sends[s][...] = rows[rank_ref[0] ^ s]
    out = dns[0][UB : UB + 16, :].astype(f32)
    for s in range(1, MP):
        out = out + dns[s][UB : UB + 16, :].astype(f32)
    out = out.astype(bf16)
    for g in range(16):
        block_ref[g * 16 : (g + 1) * 16, :] = out[:, g * 64 : (g + 1) * 64]


def fm_back_call(rank, dns, recv, projpad, normed, inv, mix):
    args = list(dns) + [recv, projpad, normed, inv, mix]
    whole = lambda shape: pl.BlockSpec(shape, lambda i, r: (0,) * len(shape))
    return pl.pallas_call(
        fm_back_kernel,
        grid_spec=pltpu.PrefetchScalarGridSpec(
            num_scalar_prefetch=1,
            grid=(1,),
            in_specs=[whole(x.shape) for x in args],
            out_specs=[whole((UB * FH, E))] * MP + [whole((U, 64))],
            scratch_shapes=[pltpu.VMEM((UB * R, E), f32), pltpu.VMEM((MP, UB * FH, E), bf16)],
        ),
        out_shape=[jax.ShapeDtypeStruct((UB * FH, E), bf16)] * MP
        + [jax.ShapeDtypeStruct((U, 64), bf16)],
        name="fm_backward",
    )(rank, *args)


def query_kernel(idx_ref, ev_ref, *refs):
    gps, (w_ref, out_ref, pooled_ref, scr, acc) = refs[:MP], refs[MP:]
    i = pl.program_id(0)
    mask = own_lanes()
    for s in range(MP):

        @pl.when(i == s)
        def _():
            pooled_ref[...] = gps[s][...]

    for u in range(UB):
        c = dot(pooled_ref[u * FH : (u + 1) * FH, :], ev_ref[u * E : (u + 1) * E, :], NT)
        scr[u : u + 1, :] = jnp.sum(jnp.where(mask, c, 0.0), axis=0, keepdims=True)
    w = w_ref[...]
    contrib = scr[...]
    d = w * (contrib - group_reduce(w * contrib, jnp.add))
    scr[...] = d
    parts = []
    for u in range(UB):
        row = jnp.broadcast_to(scr[u : u + 1, :], (FH, E))
        parts.append(jnp.where(mask, row, 0.0).astype(bf16))
    term = dot(jnp.concatenate(parts, axis=1), ev_ref[...])

    @pl.when(i == 0)
    def _():
        acc[...] = term

    @pl.when(i > 0)
    def _():
        acc[...] += term

    @pl.when(i == pl.num_programs(0) - 1)
    def _():
        out_ref[...] = acc[...] * (1.0 / math.sqrt(E))


def query_call(idx, ev, gps, w):
    return pl.pallas_call(
        query_kernel,
        grid_spec=pltpu.PrefetchScalarGridSpec(
            num_scalar_prefetch=1,
            grid=(MP,),
            in_specs=[pl.BlockSpec((UB * E, E), lambda i, t: (t[i], 0))]
            + [pl.BlockSpec((UB * FH, E), lambda i, t: (0, 0))] * MP
            + [pl.BlockSpec((UB, E), lambda i, t: (t[i], 0))],
            out_specs=[
                pl.BlockSpec((FH, E), lambda i, t: (0, 0)),
                pl.BlockSpec((UB * FH, E), lambda i, t: (t[i], 0)),
            ],
            scratch_shapes=[pltpu.VMEM((UB, E), f32), pltpu.VMEM((FH, E), f32)],
        ),
        out_shape=[
            jax.ShapeDtypeStruct((FH, E), f32),
            jax.ShapeDtypeStruct((U * FH, E), bf16),
        ],
        name="query_gradient",
    )(idx, ev, *gps, w)


CHUNK = (192, 1024)
HALVES = [jax.ShapeDtypeStruct((1024, 2048), f32), jax.ShapeDtypeStruct((2048, 512), f32)]


def half_kernel(half_ref, stack_ref, *refs):
    part = stack_ref[0]
    up_ref, down_ref = refs[-2:]
    up_ref[...] = part[0:E].astype(f32)
    down_ref[0:64, :] = part[E:, 0:512].astype(f32)
    down_ref[64:128, :] = part[E:, 512:1024].astype(f32)


def half_call(half, stack, outs=()):
    return pl.pallas_call(
        half_kernel,
        grid_spec=pltpu.PrefetchScalarGridSpec(
            num_scalar_prefetch=1,
            grid=(8,),
            in_specs=[pl.BlockSpec((1,) + CHUNK, lambda i, t: (i, 0, 0))]
            + [pl.BlockSpec(memory_space=pl.ANY)] * len(outs),
            out_specs=[
                pl.BlockSpec((E, 1024), lambda i, t: (i, t[0])),
                pl.BlockSpec((E, 512), lambda i, t: (t[0] * 8 + i, 0)),
            ],
        ),
        out_shape=HALVES,
        input_output_aliases={2: 0, 3: 1} if outs else {},
        name="other_half" if outs else "own_half",
    )(half, stack, *outs)


SAME_CORE = [[2 * i + c for i in range(8)] for c in range(2)]


def dp_exchange(x):
    return lax.all_to_all(x, "dp", 0, 0, axis_index_groups=SAME_CORE, tiled=True)


def core_swap(x):
    return lax.ppermute(x, "dp", [(i, i ^ 1) for i in range(16)])


def exchange_slots(xs):
    return [xs[0]] + [
        lax.ppermute(xs[s], "mp", [(i, i ^ s) for i in range(MP)]) for s in range(1, MP)
    ]


def exchange(x):
    return lax.all_to_all(x, "mp", 0, 0, tiled=True)


def device_step(events, lengths, query_vecs, fm_proj, up_weight, down_weight, cotangent):
    c = lax.axis_index("dp") % 2
    m = lax.axis_index("mp")
    ev = events.reshape(U * FH * L, E)
    send, weights = pool_call(ev, lengths, query_vecs, cotangent)
    recv = exchange(send)
    projt = jnp.pad(fm_proj.T, ((0, 8), (0, 0)))
    projpad = jnp.pad(jnp.concatenate([fm_proj, fm_proj], axis=1), ((0, 0), (0, E - 2 * R)))
    rows, normed, inv, mix, cot_full = fm_call(recv, projt)
    n = exchange(rows).reshape(U, E * R)

    other = (1 - c)[None].astype(jnp.int32)
    mine = c[None].astype(jnp.int32)
    rank = m[None].astype(jnp.int32)
    slots = (m ^ jnp.arange(MP)).astype(jnp.int32)
    layer = (rank, n, cot_full, up_weight, down_weight)
    g_other, out_part, dn_part = layer_call(other * STEPS, *layer)
    got = core_swap(g_other)
    g_mine, *dn_sends = layer_call(mine * STEPS, *layer, (out_part, dn_part))
    pair = (g_mine.astype(f32) + got.astype(f32)).astype(bf16)
    parts = dp_exchange(pair)

    dns = exchange_slots(dn_sends)
    *gp_sends, block_out = fm_back_call(rank, dns, recv, projpad, normed, inv, mix)

    chunk = jnp.sum(parts.astype(f32), axis=0).astype(bf16)
    stack = dp_exchange(jnp.broadcast_to(chunk[None], (8,) + CHUNK))

    gps = exchange_slots(gp_sends)
    query_term, grad_pooled = query_call(slots, ev, gps, weights)
    grad_pooled = grad_pooled.reshape(U, FH, E)
    q_all = lax.all_to_all(
        jnp.broadcast_to(query_term.astype(bf16)[None], (16, FH, E)), "dp", 0, 0, tiled=True
    )
    grad_query = jnp.sum(q_all.astype(f32), axis=0)

    stack_other = core_swap(stack)
    halves = half_call(mine, stack)
    grad_up, grad_down = half_call(other, stack_other, halves)
    return (block_out, grad_up, grad_down, grad_pooled, grad_query)


def solution(mesh):
    in_specs = (
        P("dp", "mp", None, None),
        P("dp", "mp"),
        P("mp", None),
        P(),
        P(None, "mp"),
        P("mp", None),
        P("dp", "mp"),
    )
    out_specs = (P("dp", "mp"), P(None, "mp"), P("mp", None), P("dp", "mp", None), P("mp", None))
    return jax.shard_map(
        device_step, mesh=mesh, in_specs=in_specs, out_specs=out_specs, check_vma=False
    )
```

time: 559 us -> 259 us (0.46); the launches traced: 550 us -> 257 us
  waiting for transfers between devices: 319 us -> 46.4 us
  matrix products: 106 us -> 0 us
  Pallas kernels: 0 us -> 67.5 us
  starting transfers between devices: 0.16 us -> 37.3 us
  between operations: 14.4 us -> 0.77 us
  blocking collectives: 77.3 us -> 90.1 us
  local copies, waits for them, and re-layouts: 18.9 us -> 8.78 us
  other arithmetic: 13.9 us -> 5.88 us
    psum x2 -> x0, waiting for transfers between devices: 156 us -> none  [the longest x1 89.5 us: per_device(): lax.psum(part_up.astype(jnp.bfloat16), 'dp').astype(jnp.float32)]
    all_gather x1 -> x0, waiting for transfers between devices: 131 us -> none  [per_device(): all_pooled = lax.all_gather(pooled, 'mp', axis=1, tiled=True)]
    dot_general x15 -> x0, matrix products: 106 us -> none  [the longest x1 42 us: per_device(): jnp.einsum('bfle,fe->bfl', events, query_vecs, preferred_element_type=jnp...]
    all_to_all x0 -> x2, blocking collectives: none -> 90.1 us  [dp_exchange(): lax.all_to_all(x, 'dp', 0, 0, axis_index_groups=SAME_CORE, tiled=True)]
    pallas_call x0 -> x8, Pallas kernels: none -> 67.5 us  [the longest x2 16.3 us: layer_call(): pl.pallas_call(body, grid_spec=pltpu.PrefetchScalarGridSpec(num_scalar_pr...]
    all_gather x1 -> x0, blocking collectives: 44.1 us -> none  [per_device(): cot_full = lax.all_gather(cotangent, 'mp', axis=1, tiled=True)]
    all_to_all x0 -> x3, waiting for transfers between devices: none -> 33.5 us  [the longest x2 27.4 us: exchange(): return lax.all_to_all(x, 'mp', 0, 0, tiled=True)]
    psum x1 -> x0, blocking collectives: 33.2 us -> none  [per_device(): lax.psum(query_term.astype(jnp.bfloat16), 'dp').astype(jnp.float32)]
  transfers between devices with their start and end apart: 4 -> 19, of which waited for: 4 -> 10; matrix products, arithmetic and copies ran while one was open for 10% -> 2% of each run, Pallas kernels for 0% -> 13%
where the time goes in v1:
time: 259 us; the launch traced here: 257 us
  blocking collectives  90.1 us (35%)
  Pallas kernels  67.5 us (26%)
  waiting for transfers between devices  46.4 us (18%)
  starting transfers between devices  37.3 us (14%)
  local copies, waits for them, and re-layouts  8.78 us (3%)
  other arithmetic  5.88 us (2%)
    all_to_all x2, blocking collectives, dp_exchange(): lax.all_to_all(x, 'dp', 0, 0, axis_index_groups=SAME_CORE, tiled=True)  90.1 us
    all_to_all x2, waiting for transfers between devices, exchange(): return lax.all_to_all(x, 'mp', 0, 0, tiled=True)  27.4 us
    ppermute x14, starting transfers between devices, exchange_slots(): lax.ppermute(xs[s], 'mp', [(i, i ^ s) for i in range(MP)])  24.8 us
    pallas_call x2, Pallas kernels, layer_call(): pl.pallas_call(body, grid_spec=pltpu.PrefetchScalarGridSpec(num_scalar_pr...  16.3 us
    pallas_call x2, Pallas kernels, half_call(): pl.pallas_call(half_kernel, grid_spec=pltpu.PrefetchScalarGridSpec(num_sc...  13.2 us
    pallas_call x1, Pallas kernels, pool_call(): pl.pallas_call(pool_kernel, grid=(MP,), in_specs=[pl.BlockSpec((UB * E, E...  13.1 us
    ppermute x14, waiting for transfers between devices, exchange_slots(): lax.ppermute(xs[s], 'mp', [(i, i ^ s) for i in range(MP)])  12.9 us
    pallas_call x1, Pallas kernels, query_call(): pl.pallas_call(query_kernel, grid_spec=pltpu.PrefetchScalarGridSpec(num_s...  12.2 us
  transfers between devices with their start and end apart: 19, of which 10 were waited for; matrix products, arithmetic and copies ran while one was open for 2% of the time, Pallas kernels for 13%

profile of v1, /device:TPU:0, one launch (start us, length us, event | category | flops | bytes accessed | tf_op | source)
XLA Modules:
  0.0 256.8 jit_solution(10505219937417985374)
XLA Ops:
  0.6 1.5 copy.24.cot_ref
  2.1 1.5 copy.23.len_ref
  3.6 13.1 %pool.1 = (bf16[8,640,128]{2,1,0:T(8,128)(2,1)}, f32[256,128]{1,0:T(8,128)}) custom-call(bf16[32768,128]{1,0:T(8,128)(2,1)} %bitcast.7, s32[256,16]{1,0:T(8,128)} %copy.23.len_ref, bf16[16,128]{1,0:T(8,128)(2,1)} %q_ref.1, bf16[256,64]{1,0:T(8,128)(2,1)} %copy.24.cot_ref), custom_call_target="tpu_custom_call" | custom-call | tf_op jit(solution)/shard_map/pool/pallas_call | solution.py:75
  16.7 5.5 %all-to-all-start = ((bf16[8,640,128]{2,1,0:T(8,128)(2,1)}), bf16[8,640,128]{2,1,0:T(8,128)(2,1)S(1)}, u32[]{:S(2)}, u32[]{:S(2)}) async-start(bf16[8,640,128]{2,1,0:T(8,128)(2,1)} %get-tuple-element.39), calls=%async_computation | async-start | bytes 2621440 | tf_op jit(solution)/shard_map/all_to_all | solution.py:439
  22.2 0.6 pad.8.projt_ref
  22.8 17.9 %all-to-all-done.recv_ref.refs_8_ = bf16[8,640,128]{2,1,0:T(8,128)(2,1)S(1)} async-done(((bf16[8,640,128]{2,1,0:T(8,128)(2,1)}), bf16[8,640,128]{2,1,0:T(8,128)(2,1)S(1)}, u32[]{:S(2)}, u32[]{:S(2)}) %all-to-all-start) | async-done | bytes 1310752 | tf_op jit(solution)/shard_map/all_to_all | solution.py:439
  40.8 1.1 copy-done.1
  41.8 5.9 %fm_forward.1 = (bf16[8,32,1024]{2,1,0:T(8,128)(2,1)}, f32[32,1024]{1,0:T(8,128)}, f32[32,128]{1,0:T(8,128)}, f32[256,128]{1,0:T(8,128)}, bf16[256,512]{1,0:T(8,128)(2,1)}) custom-call(bf16[8,640,128]{2,1,0:T(8,128)(2,1)} %copy-done.1, bf16[16,128]{1,0:T(8,128)(2,1)} %pad.8.projt_ref), custom_call_target="tpu_custom_call" | custom-call | tf_op jit(solution)/shard_map/fm_forward/pallas_call | solution.py:145
  47.7 3.5 %all-to-all-start.1 = ((bf16[8,32,1024]{2,1,0:T(8,128)(2,1)}), bf16[8,32,1024]{2,1,0:T(8,128)(2,1)S(1)}, u32[]{:S(2)}, u32[]{:S(2)}) async-start(bf16[8,32,1024]{2,1,0:T(8,128)(2,1)} %get-tuple-element.40), calls=%async_computation.1 | async-start | bytes 1048576 | tf_op jit(solution)/shard_map/all_to_all | solution.py:439
  51.3 9.4 %all-to-all-done.1 = bf16[8,32,1024]{2,1,0:T(8,128)(2,1)S(1)} async-done(((bf16[8,32,1024]{2,1,0:T(8,128)(2,1)}), bf16[8,32,1024]{2,1,0:T(8,128)(2,1)S(1)}, u32[]{:S(2)}, u32[]{:S(2)}) %all-to-all-start.1) | async-done | bytes 524320 | tf_op jit(solution)/shard_map/all_to_all | solution.py:439
  60.7 0.8 copy-done.2
  61.5 7.9 %layer_first.1 = (bf16[8,192,1024]{2,1,0:T(8,128)(2,1)}, f32[256,512]{1,0:T(8,128)}, f32[256,1024]{1,0:T(8,128)}) custom-call(s32[1]{0:T(128)S(6)} %mul.7.base_ref, s32[1]{0:T(128)} %bitcast.rank_ref, bf16[256,1024]{1,0:T(8,128)(2,1)} %bitcast.9, bf16[256,512]{1,0:T(8,128)(2,1)} %get-tuple-element.41.cot_ref, bf16[1024,2048]{1,0:T(8,128)(2,1)} %up_ref.3, ...), custom_call_target="tpu_custom_call" | custom-call | tf_op jit(solution)/shard_map/layer_first/pallas_call | solution.py:247
  69.4 0.0 collective-permute-start.7
  69.4 8.4 %layer_second.1 = (bf16[8,192,1024]{2,1,0:T(8,128)(2,1)}, bf16[48,1024]{1,0:T(8,128)(2,1)}, bf16[48,1024]{1,0:T(8,128)(2,1)}, bf16[48,1024]{1,0:T(8,128)(2,1)}, ...) custom-call(s32[1]{0:T(128)S(6)} %mul.6.base_ref, ...), custom_call_target="tpu_custom_call" | custom-call | tf_op jit(solution)/shard_map/layer_second/pallas_call | solution.py:247
  77.8 0.0 collective-permute-done.7
  77.8 3.4 %add_convert_fusion = bf16[8,192,1024]{2,1,0:T(8,128)(2,1)S(1)} fusion(bf16[8,192,1024]{2,1,0:T(8,128)(2,1)S(1)} %collective-permute-done.7, bf16[8,192,1024]{2,1,0:T(8,128)(2,1)} %get-tuple-element.56), kind=kLoop, calls=%fused_computation | loop fusion | flops 6291456 | bytes 9437184 | tf_op jit(solution)/shard_map/convert_element_type | solution.py:461
  81.3 47.4 %all_to_all.25 = bf16[8,192,1024]{2,1,0:T(8,128)(2,1)S(1)} all-to-all(bf16[8,192,1024]{2,1,0:T(8,128)(2,1)S(1)} %add_convert_fusion), channel_id=1, replica_groups={{0,16,32,48,64,80,96,112},{8,24,40,56,72,88,104,120},{1,17,33,49,65,81,..., dimensions={0} | all-to-all | bytes 6291456 | tf_op jit(solution)/shard_map/all_to_all | solution.py:425
  128.7 0.6 reduce_sum.21
  129.3 0.4 broadcast_in_dim.24
  129.7 42.7 %all_to_all.26.stack_ref = bf16[8,192,1024]{2,1,0:T(8,128)(2,1)S(1)} all-to-all(bf16[8,192,1024]{2,1,0:T(8,128)(2,1)S(1)} %broadcast_in_dim.24), channel_id=1, replica_groups={{0,16,32,48,64,80,96,112},{8,24,40,56,72,88,104,120},{1,17,33,49,65,81,..., dimensions={0} | all-to-all | bytes 6291456 | tf_op jit(solution)/shard_map/all_to_all | solution.py:425
  172.4 0.0 collective-permute-start.8
  172.4 0.0 copy-done.12
  172.4 0.7 collective-permute-start
  173.1 0.6 collective-permute-start.1
  173.7 2.3 collective-permute-start.2
  176.0 0.9 collective-permute-start.3
  176.8 1.3 collective-permute-done.refs_1_
  178.2 1.4 collective-permute-start.4
  179.6 1.2 collective-permute-done.1.refs_2_
  180.8 1.1 collective-permute-start.5
  181.8 0.0 collective-permute-done.2.refs_3_
  181.9 4.2 %collective-permute-start.6 = (bf16[48,1024]{1,0:T(8,128)(2,1)}, bf16[48,1024]{1,0:T(8,128)(2,1)}, u32[]{:S(2)}, u32[]{:S(2)}) collective-permute-start(bf16[48,1024]{1,0:T(8,128)(2,1)} %get-tuple-element.51), channel_id=1, source_target_pairs={{0,7},{1,6},{2,5},{3,4},{4,3},{5,2},{6,1},{7,0},{8,15},{9,14},{10,... | collective-permute-start | bytes 294920 | tf_op jit(solution)/shard_map/ppermute | solution.py:434
  186.0 0.1 copy.25
  186.1 0.6 pad.9.refs_9_
  186.8 0.0 collective-permute-done.3.refs_4_
  186.8 0.0 collective-permute-done.4.refs_5_
  186.8 2.4 collective-permute-done.5.refs_6_
  189.2 0.0 collective-permute-done.6.refs_7_
  189.2 6.9 %fm_backward.1 = (bf16[512,128]{1,0:T(8,128)(2,1)}, bf16[512,128]{1,0:T(8,128)(2,1)}, bf16[512,128]{1,0:T(8,128)(2,1)}, bf16[512,128]{1,0:T(8,128)(2,1)}, bf16[5...) custom-call(s32[1]{0:T(128)} %bitcast.rank_ref, ...), custom_call_target="tpu_custom_call" | custom-call | tf_op jit(solution)/shard_map/fm_backward/pallas_call | solution.py:316
  196.1 1.4 collective-permute-start.9
  197.5 0.0 collective-permute-start.10
  197.5 2.2 collective-permute-start.11
  199.7 2.4 collective-permute-start.12
  202.0 0.1 collective-permute-done.9.refs_1_
  202.1 2.9 %collective-permute-start.13 = (bf16[512,128]{1,0:T(8,128)(2,1)}, bf16[512,128]{1,0:T(8,128)(2,1)}, u32[]{:S(2)}, u32[]{:S(2)}) collective-permute-start(bf16[512,128]{1,0:T(8,128)(2,1)} %get-tuple-element.67), channel_id=1, source_target_pairs={{0,5},{1,4},{2,7},{3,6},{4,1},{5,0},{6,3},{7,2},{8,13},{9,12},{10,... | collective-permute-start | bytes 393224 | tf_op jit(solution)/shard_map/ppermute | solution.py:434
  205.0 2.3 collective-permute-done.10.refs_2_
  207.3 3.7 %collective-permute-start.14 = (bf16[512,128]{1,0:T(8,128)(2,1)}, bf16[512,128]{1,0:T(8,128)(2,1)}, u32[]{:S(2)}, u32[]{:S(2)}) collective-permute-start(bf16[512,128]{1,0:T(8,128)(2,1)} %get-tuple-element.68), channel_id=1, source_target_pairs={{0,6},{1,7},{2,4},{3,5},{4,2},{5,3},{6,0},{7,1},{8,14},{9,15},{10,... | collective-permute-start | bytes 393224 | tf_op jit(solution)/shard_map/ppermute | solution.py:434
  211.0 0.0 collective-permute-done.11.refs_3_
  211.0 1.3 collective-permute-start.15
  212.2 0.5 iota_xor_fusion.idx_ref
  212.7 0.0 collective-permute-done.12.refs_4_
  212.7 0.0 collective-permute-done.13.refs_5_
  212.8 2.1 collective-permute-done.14.refs_6_
  214.9 3.5 %collective-permute-done.15.refs_7_ = bf16[512,128]{1,0:T(8,128)(2,1)} collective-permute-done((bf16[512,128]{1,0:T(8,128)(2,1)}, bf16[512,128]{1,0:T(8,128)(2,1)}, u32[]{:S(2)}, u32[]{:S(2)}) %collective-permute-start.15) | collective-permute-done | bytes 131104 | tf_op jit(solution)/shard_map/ppermute | solution.py:434
  218.4 12.2 %query_gradient.1 = (f32[16,128]{1,0:T(8,128)}, bf16[4096,128]{1,0:T(8,128)(2,1)}) custom-call(s32[8]{0:T(128)} %iota_xor_fusion.idx_ref, bf16[32768,128]{1,0:T(8,128)(2,1)} %bitcast.8, bf16[512,128]{1,0:T(8,128)(2,1)} %get-tuple-element.62.refs_0_, bf16[512,128]{1,0:T(8,128)(2,1)} %copy-done.3, bf16[512,128]{1,0:T(8,128)(2,1)} %copy-done.4, ...), custom_call_target="tpu_custom_call" | custom-call | tf_op jit(solution)/shard_map/query_gradient/pallas_call | solution.py:368
  230.6 0.7 convert_element_type.24
  231.3 0.6 broadcast_in_dim.25
  231.9 3.5 %all-to-all-start.4 = ((bf16[16,16,128]{2,1,0:T(8,128)(2,1)}), bf16[16,16,128]{2,1,0:T(8,128)(2,1)S(1)}, u32[]{:S(2)}, u32[]{:S(2)}) async-start(bf16[16,16,128]{2,1,0:T(8,128)(2,1)} %broadcast_in_dim.25), calls=%async_computation.4 | async-start | bytes 131072 | tf_op jit(solution)/shard_map/all_to_all | solution.py:473
  235.4 1.5 copy.26
  236.9 6.1 %all-to-all-done.4 = bf16[16,16,128]{2,1,0:T(8,128)(2,1)S(1)} async-done(((bf16[16,16,128]{2,1,0:T(8,128)(2,1)}), bf16[16,16,128]{2,1,0:T(8,128)(2,1)S(1)}, u32[]{:S(2)}, u32[]{:S(2)}) %all-to-all-start.4) | async-done | bytes 65568 | tf_op jit(solution)/shard_map/all_to_all | solution.py:473
  243.0 0.6 convert_reduce_fusion
  243.6 6.6 %own_half.1 = (f32[1024,2048]{1,0:T(8,128)}, f32[2048,512]{1,0:T(8,128)}) custom-call(s32[1]{0:T(128)} %bitcast.1.half_ref, bf16[8,192,1024]{2,1,0:T(8,128)(2,1)} %copy-done), custom_call_target="tpu_custom_call" | custom-call | tf_op jit(solution)/shard_map/own_half/pallas_call | solution.py:403
  250.2 0.0 collective-permute-done.8.stack_ref
  250.2 6.6 %other_half.1 = (f32[1024,2048]{1,0:T(8,128)}, f32[2048,512]{1,0:T(8,128)}) custom-call(s32[1]{0:T(128)} %bitcast.5.half_ref, bf16[8,192,1024]{2,1,0:T(8,128)(2,1)} %collective-permute-done.8.stack_ref, f32[1024,2048]{1,0:T(8,128)} %get-tuple-element.58.refs_0_, f32[2048,512]{1,0:T(8,128)} %get-tuple-element.59.refs_1_), custom_call_target="tpu_custom_call", output_to_operand_aliasing={{0}: (2, {}), {1}: (3, {})} | custom-call | tf_op jit(solution)/shard_map/other_half/pallas_call | solution.py:403
  (24 shorter events, 0.0 us)
Async XLA Ops:
  3.6 18.6 %copy-start.9 = (bf16[128,8]{0,1:T(8,128)(2,1)S(1)}, bf16[128,8]{0,1:T(8,128)(2,1)}, u32[]{:S(2)}) copy-start(bf16[128,8]{0,1:T(8,128)(2,1)} %param.10) | copy-start | bytes 6148
  16.7 24.1 %all-to-all-start = ((bf16[8,640,128]{2,1,0:T(8,128)(2,1)}), bf16[8,640,128]{2,1,0:T(8,128)(2,1)S(1)}, u32[]{:S(2)}, u32[]{:S(2)}) async-start(bf16[8,640,128]{2,1,0:T(8,128)(2,1)} %get-tuple-element.39), calls=%async_computation | async-start | bytes 2621440 | tf_op jit(solution)/shard_map/all_to_all | solution.py:439
  40.8 1.1 copy-start.1
  47.7 13.0 %all-to-all-start.1 = ((bf16[8,32,1024]{2,1,0:T(8,128)(2,1)}), bf16[8,32,1024]{2,1,0:T(8,128)(2,1)S(1)}, u32[]{:S(2)}, u32[]{:S(2)}) async-start(bf16[8,32,1024]{2,1,0:T(8,128)(2,1)} %get-tuple-element.40), calls=%async_computation.1 | async-start | bytes 1048576 | tf_op jit(solution)/shard_map/all_to_all | solution.py:439
  60.7 0.8 copy-start.2
  69.4 8.4 %collective-permute-start.7 = (bf16[8,192,1024]{2,1,0:T(8,128)(2,1)}, bf16[8,192,1024]{2,1,0:T(8,128)(2,1)S(1)}, u32[]{:S(2)}, u32[]{:S(2)}) collective-permute-start(bf16[8,192,1024]{2,1,0:T(8,128)(2,1)} %get-tuple-element.57), channel_id=1, source_target_pairs={{0,8},{8,0},{16,24},{24,16},{32,40},{40,32},{48,56},{56,48},{64,72... | collective-permute-start | bytes 9437192 | tf_op jit(solution)/shard_map/ppermute | solution.py:429
  129.7 42.7 %copy-start.12 = (bf16[48,1024]{1,0:T(8,128)(2,1)S(1)}, bf16[48,1024]{1,0:T(8,128)(2,1)}, u32[]{:S(2)}) copy-start(bf16[48,1024]{1,0:T(8,128)(2,1)} %get-tuple-element.45) | copy-start | bytes 294916
  129.7 43.4 %copy-start.11 = (bf16[48,1024]{1,0:T(8,128)(2,1)S(1)}, bf16[48,1024]{1,0:T(8,128)(2,1)}, u32[]{:S(2)}) copy-start(bf16[48,1024]{1,0:T(8,128)(2,1)} %get-tuple-element.46) | copy-start | bytes 294916
  129.7 44.0 %copy-start.10 = (bf16[48,1024]{1,0:T(8,128)(2,1)S(1)}, bf16[48,1024]{1,0:T(8,128)(2,1)}, u32[]{:S(2)}) copy-start(bf16[48,1024]{1,0:T(8,128)(2,1)} %get-tuple-element.47) | copy-start | bytes 294916
  172.4 58.2 %copy-start = (bf16[8,192,1024]{2,1,0:T(8,128)(2,1)}, bf16[8,192,1024]{2,1,0:T(8,128)(2,1)S(1)}, u32[]{:S(2)}) copy-start(bf16[8,192,1024]{2,1,0:T(8,128)(2,1)S(1)} %all_to_all.26.stack_ref) | copy-start | bytes 9437188
  172.4 77.8 %collective-permute-start.8 = (bf16[8,192,1024]{2,1,0:T(8,128)(2,1)S(1)}, bf16[8,192,1024]{2,1,0:T(8,128)(2,1)}, u32[]{:S(2)}, u32[]{:S(2)}) collective-permute-start(bf16[8,192,1024]{2,1,0:T(8,128)(2,1)S(1)} %all_to_all.26.stack_ref), channel_id=1, source_target_pairs={{0,8},{8,0},{16,24},{24,16},{32,40},{40,32},{48,56},{56,48},{64,72... | collective-permute-start | bytes 9437192 | tf_op jit(solution)/shard_map/ppermute | solution.py:429
  172.4 5.7 %collective-permute-start = (bf16[48,1024]{1,0:T(8,128)(2,1)S(1)}, bf16[48,1024]{1,0:T(8,128)(2,1)S(1)}, u32[]{:S(2)}, u32[]{:S(2)}) collective-permute-start(bf16[48,1024]{1,0:T(8,128)(2,1)S(1)} %copy-done.12), channel_id=1, source_target_pairs={{0,1},{1,0},{2,3},{3,2},{4,5},{5,4},{6,7},{7,6},{8,9},{9,8},{10,11... | collective-permute-start | bytes 294920 | tf_op jit(solution)/shard_map/ppermute | solution.py:434
  173.1 7.6 %collective-permute-start.1 = (bf16[48,1024]{1,0:T(8,128)(2,1)S(1)}, bf16[48,1024]{1,0:T(8,128)(2,1)S(1)}, u32[]{:S(2)}, u32[]{:S(2)}) collective-permute-start(bf16[48,1024]{1,0:T(8,128)(2,1)S(1)} %copy-done.11), channel_id=1, source_target_pairs={{0,2},{1,3},{2,0},{3,1},{4,6},{5,7},{6,4},{7,5},{8,10},{9,11},{10,... | collective-permute-start | bytes 294920 | tf_op jit(solution)/shard_map/ppermute | solution.py:434
  173.7 8.1 %collective-permute-start.2 = (bf16[48,1024]{1,0:T(8,128)(2,1)S(1)}, bf16[48,1024]{1,0:T(8,128)(2,1)S(1)}, u32[]{:S(2)}, u32[]{:S(2)}) collective-permute-start(bf16[48,1024]{1,0:T(8,128)(2,1)S(1)} %copy-done.10), channel_id=1, source_target_pairs={{0,3},{1,2},{2,1},{3,0},{4,7},{5,6},{6,5},{7,4},{8,11},{9,10},{10,... | collective-permute-start | bytes 294920 | tf_op jit(solution)/shard_map/ppermute | solution.py:434
  176.0 10.8 %collective-permute-start.3 = (bf16[48,1024]{1,0:T(8,128)(2,1)}, bf16[48,1024]{1,0:T(8,128)(2,1)}, u32[]{:S(2)}, u32[]{:S(2)}) collective-permute-start(bf16[48,1024]{1,0:T(8,128)(2,1)} %get-tuple-element.48), channel_id=1, source_target_pairs={{0,4},{1,5},{2,6},{3,7},{4,0},{5,1},{6,2},{7,3},{8,12},{9,13},{10,... | collective-permute-start | bytes 294920 | tf_op jit(solution)/shard_map/ppermute | solution.py:434
  178.2 11.1 %copy-start.6 = (bf16[48,1024]{1,0:T(8,128)(2,1)}, bf16[48,1024]{1,0:T(8,128)(2,1)S(1)}, u32[]{:S(2)}) copy-start(bf16[48,1024]{1,0:T(8,128)(2,1)S(1)} %collective-permute-done.refs_1_) | copy-start | bytes 294916
  178.2 8.6 %collective-permute-start.4 = (bf16[48,1024]{1,0:T(8,128)(2,1)}, bf16[48,1024]{1,0:T(8,128)(2,1)}, u32[]{:S(2)}, u32[]{:S(2)}) collective-permute-start(bf16[48,1024]{1,0:T(8,128)(2,1)} %get-tuple-element.49), channel_id=1, source_target_pairs={{0,5},{1,4},{2,7},{3,6},{4,1},{5,0},{6,3},{7,2},{8,13},{9,12},{10,... | collective-permute-start | bytes 294920 | tf_op jit(solution)/shard_map/ppermute | solution.py:434
  180.8 8.5 %copy-start.7 = (bf16[48,1024]{1,0:T(8,128)(2,1)}, bf16[48,1024]{1,0:T(8,128)(2,1)S(1)}, u32[]{:S(2)}) copy-start(bf16[48,1024]{1,0:T(8,128)(2,1)S(1)} %collective-permute-done.1.refs_2_) | copy-start | bytes 294916
  180.8 8.5 %collective-permute-start.5 = (bf16[48,1024]{1,0:T(8,128)(2,1)}, bf16[48,1024]{1,0:T(8,128)(2,1)}, u32[]{:S(2)}, u32[]{:S(2)}) collective-permute-start(bf16[48,1024]{1,0:T(8,128)(2,1)} %get-tuple-element.50), channel_id=1, source_target_pairs={{0,6},{1,7},{2,4},{3,5},{4,2},{5,3},{6,0},{7,1},{8,14},{9,15},{10,... | collective-permute-start | bytes 294920 | tf_op jit(solution)/shard_map/ppermute | solution.py:434
  181.8 7.4 %copy-start.8 = (bf16[48,1024]{1,0:T(8,128)(2,1)}, bf16[48,1024]{1,0:T(8,128)(2,1)S(1)}, u32[]{:S(2)}) copy-start(bf16[48,1024]{1,0:T(8,128)(2,1)S(1)} %collective-permute-done.2.refs_3_) | copy-start | bytes 294916
  181.9 7.4 %collective-permute-start.6 = (bf16[48,1024]{1,0:T(8,128)(2,1)}, bf16[48,1024]{1,0:T(8,128)(2,1)}, u32[]{:S(2)}, u32[]{:S(2)}) collective-permute-start(bf16[48,1024]{1,0:T(8,128)(2,1)} %get-tuple-element.51), channel_id=1, source_target_pairs={{0,7},{1,6},{2,5},{3,4},{4,3},{5,2},{6,1},{7,0},{8,15},{9,14},{10,... | collective-permute-start | bytes 294920 | tf_op jit(solution)/shard_map/ppermute | solution.py:434
  196.1 6.0 %collective-permute-start.9 = (bf16[512,128]{1,0:T(8,128)(2,1)}, bf16[512,128]{1,0:T(8,128)(2,1)S(1)}, u32[]{:S(2)}, u32[]{:S(2)}) collective-permute-start(bf16[512,128]{1,0:T(8,128)(2,1)} %get-tuple-element.63), channel_id=1, source_target_pairs={{0,1},{1,0},{2,3},{3,2},{4,5},{5,4},{6,7},{7,6},{8,9},{9,8},{10,11... | collective-permute-start | bytes 393224 | tf_op jit(solution)/shard_map/ppermute | solution.py:434
  197.5 9.8 %collective-permute-start.10 = (bf16[512,128]{1,0:T(8,128)(2,1)}, bf16[512,128]{1,0:T(8,128)(2,1)S(1)}, u32[]{:S(2)}, u32[]{:S(2)}) collective-permute-start(bf16[512,128]{1,0:T(8,128)(2,1)} %get-tuple-element.64), channel_id=1, source_target_pairs={{0,2},{1,3},{2,0},{3,1},{4,6},{5,7},{6,4},{7,5},{8,10},{9,11},{10,... | collective-permute-start | bytes 393224 | tf_op jit(solution)/shard_map/ppermute | solution.py:434
  197.5 13.5 %collective-permute-start.11 = (bf16[512,128]{1,0:T(8,128)(2,1)}, bf16[512,128]{1,0:T(8,128)(2,1)S(1)}, u32[]{:S(2)}, u32[]{:S(2)}) collective-permute-start(bf16[512,128]{1,0:T(8,128)(2,1)} %get-tuple-element.65), channel_id=1, source_target_pairs={{0,3},{1,2},{2,1},{3,0},{4,7},{5,6},{6,5},{7,4},{8,11},{9,10},{10,... | collective-permute-start | bytes 393224 | tf_op jit(solution)/shard_map/ppermute | solution.py:434
  199.7 13.1 %collective-permute-start.12 = (bf16[512,128]{1,0:T(8,128)(2,1)}, bf16[512,128]{1,0:T(8,128)(2,1)}, u32[]{:S(2)}, u32[]{:S(2)}) collective-permute-start(bf16[512,128]{1,0:T(8,128)(2,1)} %get-tuple-element.66), channel_id=1, source_target_pairs={{0,4},{1,5},{2,6},{3,7},{4,0},{5,1},{6,2},{7,3},{8,12},{9,13},{10,... | collective-permute-start | bytes 393224 | tf_op jit(solution)/shard_map/ppermute | solution.py:434
  202.1 16.3 %copy-start.3 = (bf16[512,128]{1,0:T(8,128)(2,1)}, bf16[512,128]{1,0:T(8,128)(2,1)S(1)}, u32[]{:S(2)}) copy-start(bf16[512,128]{1,0:T(8,128)(2,1)S(1)} %collective-permute-done.9.refs_1_) | copy-start | bytes 393220
  202.1 10.7 %collective-permute-start.13 = (bf16[512,128]{1,0:T(8,128)(2,1)}, bf16[512,128]{1,0:T(8,128)(2,1)}, u32[]{:S(2)}, u32[]{:S(2)}) collective-permute-start(bf16[512,128]{1,0:T(8,128)(2,1)} %get-tuple-element.67), channel_id=1, source_target_pairs={{0,5},{1,4},{2,7},{3,6},{4,1},{5,0},{6,3},{7,2},{8,13},{9,12},{10,... | collective-permute-start | bytes 393224 | tf_op jit(solution)/shard_map/ppermute | solution.py:434
  207.3 11.1 %copy-start.4 = (bf16[512,128]{1,0:T(8,128)(2,1)}, bf16[512,128]{1,0:T(8,128)(2,1)S(1)}, u32[]{:S(2)}) copy-start(bf16[512,128]{1,0:T(8,128)(2,1)S(1)} %collective-permute-done.10.refs_2_) | copy-start | bytes 393220
  207.3 7.6 %collective-permute-start.14 = (bf16[512,128]{1,0:T(8,128)(2,1)}, bf16[512,128]{1,0:T(8,128)(2,1)}, u32[]{:S(2)}, u32[]{:S(2)}) collective-permute-start(bf16[512,128]{1,0:T(8,128)(2,1)} %get-tuple-element.68), channel_id=1, source_target_pairs={{0,6},{1,7},{2,4},{3,5},{4,2},{5,3},{6,0},{7,1},{8,14},{9,15},{10,... | collective-permute-start | bytes 393224 | tf_op jit(solution)/shard_map/ppermute | solution.py:434
  211.0 7.4 %copy-start.5 = (bf16[512,128]{1,0:T(8,128)(2,1)}, bf16[512,128]{1,0:T(8,128)(2,1)S(1)}, u32[]{:S(2)}) copy-start(bf16[512,128]{1,0:T(8,128)(2,1)S(1)} %collective-permute-done.11.refs_3_) | copy-start | bytes 393220
  211.0 7.4 %collective-permute-start.15 = (bf16[512,128]{1,0:T(8,128)(2,1)}, bf16[512,128]{1,0:T(8,128)(2,1)}, u32[]{:S(2)}, u32[]{:S(2)}) collective-permute-start(bf16[512,128]{1,0:T(8,128)(2,1)} %get-tuple-element.69), channel_id=1, source_target_pairs={{0,7},{1,6},{2,5},{3,4},{4,3},{5,2},{6,1},{7,0},{8,15},{9,14},{10,... | collective-permute-start | bytes 393224 | tf_op jit(solution)/shard_map/ppermute | solution.py:434
  231.9 11.1 %all-to-all-start.4 = ((bf16[16,16,128]{2,1,0:T(8,128)(2,1)}), bf16[16,16,128]{2,1,0:T(8,128)(2,1)S(1)}, u32[]{:S(2)}, u32[]{:S(2)}) async-start(bf16[16,16,128]{2,1,0:T(8,128)(2,1)} %broadcast_in_dim.25), calls=%async_computation.4 | async-start | bytes 131072 | tf_op jit(solution)/shard_map/all_to_all | solution.py:473

commit v2 on v1

v2 whole, which is shorter than its diff:
```python
import math

import jax
import jax.numpy as jnp
from jax import lax
from jax.experimental import pallas as pl
from jax.experimental.pallas import tpu as pltpu
from jax.sharding import PartitionSpec as P


norm_eps = 1e-05
f32 = jnp.float32
bf16 = jnp.bfloat16


E = 128
L = 8
R = 8
MP = 8
FH = 16
UB = 32
U = 256
NT = (((1,), (1,)), ((), ()))
TN = (((0,), (0,)), ((), ()))
NN = (((1,), (0,)), ((), ()))


def dot(a, b, dims=NN):
    return lax.dot_general(a, b, dims, preferred_element_type=f32)


def iota(shape, axis):
    return lax.broadcasted_iota(jnp.int32, shape, axis)


def own_lanes():
    return iota((FH, E), 0) == iota((FH, E), 1) // L


def group_reduce(x, op):
    lane = iota(x.shape, 1)
    for s in (1, 2, 4):
        up = pltpu.roll(x, E - s, 1)
        down = pltpu.roll(x, s, 1)
        x = op(x, jnp.where((lane & s) == 0, up, down))
    return x


PARTS = 4
PER = MP // PARTS


def pool_kernel(
    ev_hbm, lent_ref, q_ref, cott_ref, send_hbm, w_hbm, ev, send, w, in_sem, out_sem, w_sem
):
    rows = PER * UB * E
    loads = [
        pltpu.make_async_copy(ev_hbm.at[pl.ds(g * rows, rows)], ev.at[g], in_sem.at[g])
        for g in range(PARTS)
    ]
    for load in loads:
        load.start()
    mask = own_lanes()
    spread = mask.astype(f32).astype(bf16)
    lens = dot(lent_ref[...].astype(f32).astype(bf16), spread, TN)
    live = (iota((U, E), 1) % L).astype(f32) < lens
    q = q_ref[...]
    for g in range(PARTS):
        loads[g].wait()
        raw = dot(q, ev[g], NT)
        for u in range(PER * UB):
            block = jnp.where(mask, raw[:, u * E : (u + 1) * E], 0.0)
            at = g * PER * UB + u
            w[at : at + 1, :] = jnp.sum(block, axis=0, keepdims=True)
    scores = w[...] * (1.0 / math.sqrt(E))
    top = group_reduce(jnp.where(live, scores, -1e30), jnp.maximum)
    ex = jnp.exp(jnp.where(live, scores - top, -1e30))
    w[...] = ex / group_reduce(ex, jnp.add)
    w_copy = pltpu.make_async_copy(w, w_hbm, w_sem)
    w_copy.start()
    stores = []
    for p in range(MP):
        for u in range(UB):
            row = jnp.broadcast_to(w[p * UB + u : p * UB + u + 1, :], (FH, E))
            mix = jnp.where(mask, row, 0.0).astype(bf16)
            at = ((p % PER) * UB + u) * E
            pooled = dot(mix, ev[p // PER, at : at + E, :])
            send[p, u * FH : (u + 1) * FH, :] = pooled.astype(bf16)
        send[p, UB * FH : UB * FH + 64, :] = cott_ref[:, 0:E]
        send[p, UB * FH + 64 :, :] = cott_ref[:, E:]
        stores.append(pltpu.make_async_copy(send.at[p], send_hbm.at[p], out_sem.at[p]))
        stores[-1].start()
    for store in stores:
        store.wait()
    w_copy.wait()


HBM = pl.BlockSpec(memory_space=pltpu.HBM)
VMEM = pl.BlockSpec(memory_space=pltpu.VMEM)


def pool_call(ev, lent, q, cott):
    rows = UB * FH + U // 2
    return pl.pallas_call(
        pool_kernel,
        in_specs=[HBM, VMEM, VMEM, VMEM],
        out_specs=[HBM, HBM],
        out_shape=[
            jax.ShapeDtypeStruct((MP, rows, E), bf16),
            jax.ShapeDtypeStruct((U, E), f32),
        ],
        scratch_shapes=[
            pltpu.VMEM((PARTS, PER * UB * E, E), bf16),
            pltpu.VMEM((MP, rows, E), bf16),
            pltpu.VMEM((U, E), f32),
            pltpu.SemaphoreType.DMA((PARTS,)),
            pltpu.SemaphoreType.DMA((MP,)),
            pltpu.SemaphoreType.DMA,
        ],
        name="pool",
    )(ev, lent, q, cott)


def flat_mask():
    return iota((E, E), 0) % FH == iota((E, E), 1) // R


def tile_ranks(m):
    pair = jnp.concatenate([m, m], axis=0).astype(bf16)
    return jnp.concatenate([pair] * 8, axis=0)


def user_rows(ref, u):
    return jnp.concatenate(
        [ref[j, pl.ds(pl.multiple_of(u * FH, FH), FH), :] for j in range(MP)], axis=0
    )


def fm_kernel(recv_ref, projt_ref, send_ref, normed_ref, inv_ref, mix_ref, cot_ref, scr):
    mask = flat_mask()
    projt = projt_ref[...]

    def step(u, carry):
        p = user_rows(recv_ref, u)
        mix = dot(projt, p)[0:R].astype(bf16).astype(f32)
        full = jnp.where(mask, dot(p, tile_ranks(mix), NT), 0.0)
        at = pl.multiple_of(u * R, R)
        mix_ref[pl.ds(at, R), :] = mix
        scr[pl.ds(at, R), :] = jnp.sum(full.reshape(MP, FH, E), axis=1)
        return carry

    lax.fori_loop(0, UB, step, 0, unroll=16)
    total = jnp.zeros((UB, 1), f32)
    for j in range(MP):
        x = scr[pl.ds(j, UB, stride=R), :]
        total = total + jnp.sum(x * x, axis=1, keepdims=True)
    inv = lax.rsqrt(total * (1.0 / (E * R)) + norm_eps)
    inv_ref[...] = jnp.broadcast_to(inv, (UB, E))
    for j in range(MP):
        x = scr[pl.ds(j, UB, stride=R), :] * inv
        normed_ref[:, j * E : (j + 1) * E] = x
        for p in range(MP):
            send_ref[p, :, j * E : (j + 1) * E] = x.astype(bf16)
    at = UB * FH
    for j in range(MP):
        cot_ref[j * 64 : (j + 1) * 64, 0:E] = recv_ref[j, at : at + 64, :]
        cot_ref[j * 64 : (j + 1) * 64, E:] = recv_ref[j, at + 64 :, :]


def fm_call(recv, projt):
    return pl.pallas_call(
        fm_kernel,
        out_shape=[
            jax.ShapeDtypeStruct((MP, UB, E * R), bf16),
            jax.ShapeDtypeStruct((UB, E * R), f32),
            jax.ShapeDtypeStruct((UB, E), f32),
            jax.ShapeDtypeStruct((UB * R, E), f32),
            jax.ShapeDtypeStruct((512, U), bf16),
        ],
        scratch_shapes=[pltpu.VMEM((UB * R, E), f32)],
        name="fm_forward",
    )(recv, projt)


HB = 256
STEPS = 4
HALF = HB * STEPS


def weight_loads(half, up_hbm, down_hbm, up, down, sem):
    loads = []
    for k in range(STEPS):
        at = pl.multiple_of(half * HALF + k * HB, HB)
        here = pl.ds(k * HB, HB)
        loads.append(
            (
                pltpu.make_async_copy(up_hbm.at[:, pl.ds(at, HB)], up.at[:, here], sem.at[0, k]),
                pltpu.make_async_copy(down_hbm.at[pl.ds(at, HB)], down.at[here], sem.at[1, k]),
            )
        )
    return loads


def start_all(copies):
    for copy in copies:
        copy.start()


def wait_all(copies):
    for copy in copies:
        copy.wait()


def layer_half(loads, n, nt, cot, up, down, act, dh, g, g_hbm, sem):
    stores = []
    for k in range(STEPS):
        wait_all(loads[k])
        cols = slice(k * HB, (k + 1) * HB)
        hidden = dot(n, up[:, cols])
        d_act = dot(cot, down[cols, :], NT)
        s = 1.0 / (1.0 + jnp.exp(-hidden))
        act_k = (hidden * s).astype(bf16)
        dh_k = (d_act * s * (1.0 + hidden * (1.0 - s))).astype(bf16)
        act[:, cols] = act_k
        dh[:, cols] = dh_k
        g[:, 0:E, cols] = dot(nt, dh_k).astype(bf16).reshape(MP, E, HB)
        g_down = dot(act_k, cot, TN).astype(bf16)
        for t in range(2):
            for h in range(2):
                at = t * 128 + h * 64
                g[2 * k + t, E:, h * 512 : (h + 1) * 512] = g_down[at : at + 64, :]
        here = pl.ds(k * HB, HB)
        pair = pl.ds(2 * k, 2)
        low = pl.ds(E, 64)
        stores += [
            pltpu.make_async_copy(
                g.at[:, pl.ds(0, E), here], g_hbm.at[:, pl.ds(0, E), here], sem.at[0, k]
            ),
            pltpu.make_async_copy(g.at[pair, low], g_hbm.at[pair, low], sem.at[1, k]),
        ]
        start_all(stores[-2:])
    return stores


def layer_first(
    half_ref, n_hbm, cott_hbm, up_hbm, down_hbm, g_hbm, act_hbm, dh_hbm,
    n, nt, cott, up, down, act, dh, g, in_sem, w_sem, g_sem, out_sem,
):
    first = [
        pltpu.make_async_copy(n_hbm, n, in_sem.at[0]),
        pltpu.make_async_copy(cott_hbm, cott, in_sem.at[1]),
    ]
    loads = weight_loads(half_ref[0], up_hbm, down_hbm, up, down, w_sem)
    start_all(first)
    for pair in loads:
        start_all(pair)
    wait_all(first)
    rows = n[...]
    nt[...] = rows.T
    cot = cott[...].T
    stores = layer_half(loads, rows, nt[...], cot, up, down, act, dh, g, g_hbm, g_sem)
    last = [
        pltpu.make_async_copy(act, act_hbm, out_sem.at[0]),
        pltpu.make_async_copy(dh, dh_hbm, out_sem.at[1]),
    ]
    start_all(last)
    wait_all(stores)
    wait_all(last)


def layer_second(
    half_ref, n_hbm, cott_hbm, up_hbm, down_hbm, act_hbm, dh_hbm, g_hbm, *refs
):
    sends = refs[:MP]
    n, nt, cott, up, down, act, dh, g, in_sem, w_sem, g_sem = refs[MP : MP + 11]
    up_o, down_o, act_o, dh_o, dn, packed, wo_sem = refs[MP + 11 :]
    first = [
        pltpu.make_async_copy(n_hbm, n, in_sem.at[0]),
        pltpu.make_async_copy(cott_hbm, cott, in_sem.at[1]),
    ]
    half = half_ref[0]
    loads = weight_loads(half, up_hbm, down_hbm, up, down, w_sem)
    others = weight_loads(1 - half, up_hbm, down_hbm, up_o, down_o, wo_sem)
    late = [
        pltpu.make_async_copy(act_hbm, act_o, in_sem.at[2]),
        pltpu.make_async_copy(dh_hbm, dh_o, in_sem.at[3]),
    ]
    for pair in others:
        late += pair
    start_all(first)
    for pair in loads:
        start_all(pair)
    start_all(late)
    wait_all(first)
    rows = n[...]
    nt[...] = rows.T
    cot = cott[...].T
    stores = layer_half(loads, rows, nt[...], cot, up, down, act, dh, g, g_hbm, g_sem)
    wait_all(late)
    out = dot(act[...], down[...]) + dot(act_o[...], down_o[...])
    out = out.T
    for p in range(MP):
        for a in range(4):
            at = p * 64 + a * 16
            packed[p, :, a * U : (a + 1) * U] = out[at : at + 16, :].astype(bf16)
    dn[...] = dot(dh[...], up[...], NT) + dot(dh_o[...], up_o[...], NT)
    for s in range(MP):
        p = half_ref[1] ^ s
        sends[s][0:UB, :] = dn[pl.ds(pl.multiple_of(p * UB, UB), UB), :].astype(bf16)
        sends[s][UB:, :] = packed[p]
    wait_all(stores)


def layer_call(half, n, cott, up, down, others=()):
    wide, tall = pltpu.VMEM((E * R, HALF), bf16), pltpu.VMEM((HALF, 512), bf16)
    slab = pltpu.VMEM((U, HALF), bf16)
    sems = lambda *shape: pltpu.SemaphoreType.DMA(shape)
    scratch = [
        pltpu.VMEM((U, E * R), bf16),
        pltpu.VMEM((E * R, U), bf16),
        pltpu.VMEM((512, U), bf16),
        wide, tall, slab, slab,
        pltpu.VMEM((MP, 192, 1024), bf16),
    ]
    g_shape = jax.ShapeDtypeStruct((MP, 192, 1024), bf16)
    if others:
        body = layer_second
        scratch += [sems(4), sems(2, STEPS), sems(2, STEPS)]
        scratch += [wide, tall, slab, slab, pltpu.VMEM((U, E * R), f32)]
        scratch += [pltpu.VMEM((MP, 16, 1024), bf16), sems(2, STEPS)]
        out_specs = [HBM] + [VMEM] * MP
        out_shape = [g_shape] + [jax.ShapeDtypeStruct((48, 1024), bf16)] * MP
    else:
        body = layer_first
        scratch += [sems(2), sems(2, STEPS), sems(2, STEPS), sems(2)]
        out_specs = [HBM] * 3
        out_shape = [g_shape] + [jax.ShapeDtypeStruct((U, HALF), bf16)] * 2
    return pl.pallas_call(
        body,
        in_specs=[pl.BlockSpec(memory_space=pltpu.SMEM)] + [HBM] * (4 + len(others)),
        out_specs=out_specs,
        out_shape=out_shape,
        scratch_shapes=scratch,
        name="layer_second" if others else "layer_first",
    )(half, n, cott, up, down, *others)


def fm_back_kernel(rank_ref, *refs):
    dns = refs[:MP]
    recv_ref, projpad_ref, normed_ref, inv_ref, mix_ref = refs[MP : MP + 5]
    sends = refs[MP + 5 : 2 * MP + 5]
    block_ref, scr, rows = refs[2 * MP + 5 :]
    mask = flat_mask()
    inv = inv_ref[...][:, 0:1]
    dots = jnp.zeros((UB, 1), f32)
    for j in range(MP):
        at = slice(j * E, (j + 1) * E)
        d = dns[0][0:UB, at].astype(f32)
        for s in range(1, MP):
            d = d + dns[s][0:UB, at].astype(f32)
        scr[pl.ds(j, UB, stride=R), :] = d
        dots = dots + jnp.sum(d * normed_ref[:, at], axis=1, keepdims=True)
    mean = dots * (1.0 / (E * R))
    for j in range(MP):
        at = slice(j * E, (j + 1) * E)
        d = scr[pl.ds(j, UB, stride=R), :]
        scr[pl.ds(j, UB, stride=R), :] = inv * (d - normed_ref[:, at] * mean)
    projpad = projpad_ref[...]

    def step(u, carry):
        at = pl.multiple_of(u * R, R)
        p = user_rows(recv_ref, u)
        g = scr[pl.ds(at, R), :]
        spread = jnp.concatenate(
            [jnp.broadcast_to(g[j : j + 1, :], (FH, E)) for j in range(MP)], axis=0
        )
        spread = jnp.where(mask, spread, 0.0).astype(bf16)
        back = jnp.sum(dot(spread, p, TN).reshape(FH, R, E), axis=0)
        high = back.astype(bf16).astype(f32)
        pair = jnp.concatenate([high, back - high], axis=0).astype(bf16)
        back_rows = jnp.concatenate([pair] * 8, axis=0)
        left = jnp.concatenate([spread, projpad], axis=1)
        right = jnp.concatenate([tile_ranks(mix_ref[pl.ds(at, R), :]), back_rows], axis=0)
        grad = dot(left, right).astype(bf16)
        for j in range(MP):
            rows[j, pl.ds(pl.multiple_of(u * FH, FH), FH), :] = grad[j * FH : (j + 1) * FH, :]
        return carry

    lax.fori_loop(0, UB, step, 0, unroll=16)
    for s in range(MP):
        sends[s][...] = rows[rank_ref[0] ^ s]
    out = dns[0][UB : UB + 16, :].astype(f32)
    for s in range(1, MP):
        out = out + dns[s][UB : UB + 16, :].astype(f32)
    out = out.astype(bf16)
    for a in range(4):
        block_ref[a * 16 : (a + 1) * 16, :] = out[:, a * U : (a + 1) * U]


def fm_back_call(rank, dns, recv, projpad, normed, inv, mix):
    args = list(dns) + [recv, projpad, normed, inv, mix]
    whole = lambda shape: pl.BlockSpec(shape, lambda i, r: (0,) * len(shape))
    return pl.pallas_call(
        fm_back_kernel,
        grid_spec=pltpu.PrefetchScalarGridSpec(
            num_scalar_prefetch=1,
            grid=(1,),
            in_specs=[whole(x.shape) for x in args],
            out_specs=[whole((UB * FH, E))] * MP + [whole((64, U))],
            scratch_shapes=[pltpu.VMEM((UB * R, E), f32), pltpu.VMEM((MP, UB * FH, E), bf16)],
        ),
        out_shape=[jax.ShapeDtypeStruct((UB * FH, E), bf16)] * MP
        + [jax.ShapeDtypeStruct((64, U), bf16)],
        name="fm_backward",
    )(rank, *args)


def query_kernel(idx_ref, ev_ref, *refs):
    gps, (w_ref, out_ref, pooled_ref, scr, acc) = refs[:MP], refs[MP:]
    i = pl.program_id(0)
    mask = own_lanes()
    for s in range(MP):

        @pl.when(i == s)
        def _():
            pooled_ref[...] = gps[s][...]

    for u in range(UB):
        c = dot(pooled_ref[u * FH : (u + 1) * FH, :], ev_ref[u * E : (u + 1) * E, :], NT)
        scr[u : u + 1, :] = jnp.sum(jnp.where(mask, c, 0.0), axis=0, keepdims=True)
    w = w_ref[...]
    contrib = scr[...]
    d = w * (contrib - group_reduce(w * contrib, jnp.add))
    scr[...] = d
    parts = []
    for u in range(UB):
        row = jnp.broadcast_to(scr[u : u + 1, :], (FH, E))
        parts.append(jnp.where(mask, row, 0.0).astype(bf16))
    term = dot(jnp.concatenate(parts, axis=1), ev_ref[...])

    @pl.when(i == 0)
    def _():
        acc[...] = term

    @pl.when(i > 0)
    def _():
        acc[...] += term

    @pl.when(i == pl.num_programs(0) - 1)
    def _():
        out_ref[...] = acc[...] * (1.0 / math.sqrt(E))


def query_call(idx, ev, gps, w):
    return pl.pallas_call(
        query_kernel,
        grid_spec=pltpu.PrefetchScalarGridSpec(
            num_scalar_prefetch=1,
            grid=(MP,),
            in_specs=[pl.BlockSpec((UB * E, E), lambda i, t: (t[i], 0))]
            + [pl.BlockSpec((UB * FH, E), lambda i, t: (0, 0))] * MP
            + [pl.BlockSpec((UB, E), lambda i, t: (t[i], 0))],
            out_specs=[
                pl.BlockSpec((FH, E), lambda i, t: (0, 0)),
                pl.BlockSpec((UB * FH, E), lambda i, t: (t[i], 0)),
            ],
            scratch_shapes=[pltpu.VMEM((UB, E), f32), pltpu.VMEM((FH, E), f32)],
        ),
        out_shape=[
            jax.ShapeDtypeStruct((FH, E), f32),
            jax.ShapeDtypeStruct((U * FH, E), bf16),
        ],
        name="query_gradient",
    )(idx, ev, *gps, w)


CHUNK = (192, 1024)
HALVES = [jax.ShapeDtypeStruct((1024, 2048), f32), jax.ShapeDtypeStruct((2048, 512), f32)]


def half_kernel(half_ref, stack_hbm, *refs):
    up_hbm, down_hbm, stack, up, down, in_sem, up_sem, down_sem = refs[-8:]
    loads = [
        pltpu.make_async_copy(stack_hbm.at[i], stack.at[i], in_sem.at[i]) for i in range(8)
    ]
    start_all(loads)
    cols = pl.ds(pl.multiple_of(half_ref[0] * HALF, HALF), HALF)
    stores = []
    for i in range(8):
        loads[i].wait()
        at = i * E
        up[at : at + E, :] = stack[i, 0:E, :].astype(f32)
        down[at : at + 64, :] = stack[i, E:, 0:512].astype(f32)
        down[at + 64 : at + E, :] = stack[i, E:, 512:].astype(f32)
        rows = pl.ds(at, E)
        out_rows = pl.ds(pl.multiple_of(half_ref[0] * HALF + at, E), E)
        stores += [
            pltpu.make_async_copy(up.at[rows], up_hbm.at[rows, cols], up_sem.at[i]),
            pltpu.make_async_copy(down.at[rows], down_hbm.at[out_rows], down_sem.at[i]),
        ]
        start_all(stores[-2:])
    wait_all(stores)


def half_call(half, stack, outs=()):
    return pl.pallas_call(
        half_kernel,
        in_specs=[pl.BlockSpec(memory_space=pltpu.SMEM)] + [HBM] * (1 + len(outs)),
        out_specs=[HBM, HBM],
        out_shape=HALVES,
        scratch_shapes=[
            pltpu.VMEM((8,) + CHUNK, bf16),
            pltpu.VMEM((1024, 1024), f32),
            pltpu.VMEM((1024, 512), f32),
        ]
        + [pltpu.SemaphoreType.DMA((8,))] * 3,
        input_output_aliases={2: 0, 3: 1} if outs else {},
        name="other_half" if outs else "own_half",
    )(half, stack, *outs)


SAME_CORE = [[2 * i + c for i in range(8)] for c in range(2)]


def dp_exchange(x):
    return lax.all_to_all(x, "dp", 0, 0, axis_index_groups=SAME_CORE, tiled=True)


def core_swap(x):
    return lax.ppermute(x, "dp", [(i, i ^ 1) for i in range(16)])


def exchange_slots(xs):
    got = [xs[0]]
    for s in range(1, MP):
        got.append(lax.ppermute(xs[s], "mp", [(i, i ^ s) for i in range(MP)]))
    return got


def dp_permute(x, s):
    pairs = [
        (h * 8 + z * 2 + c, (h ^ (s // 4)) * 8 + ((z + s) % 4) * 2 + c)
        for h in range(2)
        for z in range(4)
        for c in range(2)
    ]
    return lax.ppermute(x, "dp", pairs)


def exchange(x):
    return lax.all_to_all(x, "mp", 0, 0, tiled=True)


def device_step(events, lengths, query_vecs, fm_proj, up_weight, down_weight, cotangent):
    c = lax.axis_index("dp") % 2
    m = lax.axis_index("mp")
    ev = events.reshape(U * FH * L, E)
    send, weights = pool_call(ev, lengths.T, query_vecs, cotangent.T)
    recv = exchange(send)
    projt = jnp.pad(fm_proj.T, ((0, 8), (0, 0)))
    projpad = jnp.pad(jnp.concatenate([fm_proj, fm_proj], axis=1), ((0, 0), (0, E - 2 * R)))
    rows, normed, inv, mix, cot_full = fm_call(recv, projt)
    n = exchange(rows).reshape(U, E * R)

    other = (1 - c)[None].astype(jnp.int32)
    mine = c[None].astype(jnp.int32)
    rank = m[None].astype(jnp.int32)
    slots = (m ^ jnp.arange(MP)).astype(jnp.int32)
    layer = (n, cot_full, up_weight, down_weight)
    g_other, *others = layer_call(other, *layer)
    got = core_swap(g_other)
    g_mine, *dn_sends = layer_call(jnp.concatenate([mine, rank]), *layer, tuple(others))
    pair = (g_mine.astype(f32) + got.astype(f32)).astype(bf16)
    parts = dp_exchange(pair)

    dns = exchange_slots(dn_sends)
    *gp_sends, block_out = fm_back_call(rank, dns, recv, projpad, normed, inv, mix)

    chunk = jnp.sum(parts.astype(f32), axis=0).astype(bf16)
    stack = dp_exchange(jnp.broadcast_to(chunk[None], (8,) + CHUNK))

    gps = exchange_slots(gp_sends)
    query_term, grad_pooled = query_call(slots, ev, gps, weights)
    grad_pooled = grad_pooled.reshape(U, FH, E)
    query_other = core_swap(query_term)
    query_pair = (query_term + query_other).astype(bf16)
    query_parts = [query_pair] + [dp_permute(query_pair, s) for s in range(1, 8)]
    grad_query = sum(x.astype(f32) for x in query_parts)

    stack_other = core_swap(stack)
    halves = half_call(mine, stack)
    grad_up, grad_down = half_call(other, stack_other, halves)
    return (block_out.T, grad_up, grad_down, grad_pooled, grad_query)


def solution(mesh):
    in_specs = (
        P("dp", "mp", None, None),
        P("dp", "mp"),
        P("mp", None),
        P(),
        P(None, "mp"),
        P("mp", None),
        P("dp", "mp"),
    )
    out_specs = (P("dp", "mp"), P(None, "mp"), P("mp", None), P("dp", "mp", None), P("mp", None))
    return jax.shard_map(
        device_step, mesh=mesh, in_specs=in_specs, out_specs=out_specs, check_vma=False
    )
```

time: 259 us -> 253 us (0.977)
  starting transfers between devices: 37.3 us -> 47.1 us
  Pallas kernels: 67.5 us -> 58.7 us
  local copies, waits for them, and re-layouts: 8.78 us -> 3.64 us
    ppermute x14 -> x21, starting transfers between devices: 24.8 us -> 37.7 us  [the longest x14 24.9 us: exchange_slots(): got.append(lax.ppermute(xs[s], 'mp', [(i, i ^ s) for i in range(MP)]))]
    pallas_call x5, Pallas kernels: 42.6 us -> 34.4 us  [the longest x2 17.1 us: layer_call(): pl.pallas_call(body, in_specs=[pl.BlockSpec(memory_space=pltpu.SMEM)] + [...]
    all_to_all x1 -> x0, waiting for transfers between devices: 6.07 us -> none  [device_step(): lax.all_to_all(jnp.broadcast_to(query_term.astype(bf16)[None], (16, FH, E...]
    unnamed x29 -> x26, local copies, waits for them, and re-layouts: 6.4 us -> 1.91 us
    ppermute x14 -> x21, waiting for transfers between devices: 12.9 us -> 16.8 us  [the longest x14 12.9 us: exchange_slots(): got.append(lax.ppermute(xs[s], 'mp', [(i, i ^ s) for i in range(MP)]))]
    all_to_all x1 -> x0, starting transfers between devices: 3.5 us -> none  [device_step(): lax.all_to_all(jnp.broadcast_to(query_term.astype(bf16)[None], (16, FH, E...]
  transfers between devices with their start and end apart: 19 -> 26, of which waited for: 10 -> 13; matrix products, arithmetic and copies ran while one was open for 2% -> 1% of each run, Pallas kernels for 13% -> 13%
where the time goes in v2:
time: 253 us; the launch traced here: 252 us
  blocking collectives  90.1 us (36%)
  Pallas kernels  58.7 us (23%)
  starting transfers between devices  47.1 us (19%)
  waiting for transfers between devices  45.5 us (18%)
  other arithmetic  6.43 us (3%)
  local copies, waits for them, and re-layouts  3.64 us (1%)
    all_to_all x2, blocking collectives, dp_exchange(): lax.all_to_all(x, 'dp', 0, 0, axis_index_groups=SAME_CORE, tiled=True)  90.1 us
    all_to_all x2, waiting for transfers between devices, exchange(): return lax.all_to_all(x, 'mp', 0, 0, tiled=True)  27.4 us
    ppermute x14, starting transfers between devices, exchange_slots(): got.append(lax.ppermute(xs[s], 'mp', [(i, i ^ s) for i in range(MP)]))  24.9 us
    pallas_call x2, Pallas kernels, layer_call(): pl.pallas_call(body, in_specs=[pl.BlockSpec(memory_space=pltpu.SMEM)] + [...  17.1 us
    ppermute x14, waiting for transfers between devices, exchange_slots(): got.append(lax.ppermute(xs[s], 'mp', [(i, i ^ s) for i in range(MP)]))  12.9 us
    ppermute x7, starting transfers between devices, dp_permute(): return lax.ppermute(x, 'dp', pairs)  12.8 us
    pallas_call x1, Pallas kernels, query_call(): pl.pallas_call(query_kernel, grid_spec=pltpu.PrefetchScalarGridSpec(num_s...  12.2 us
    pallas_call x1, Pallas kernels, pool_call(): pl.pallas_call(pool_kernel, in_specs=[HBM, VMEM, VMEM, VMEM], out_specs=[...  9.5 us
  transfers between devices with their start and end apart: 26, of which 13 were waited for; matrix products, arithmetic and copies ran while one was open for 1% of the time, Pallas kernels for 13%

profile of v2, /device:TPU:0, one launch (start us, length us, event | category | flops | bytes accessed | tf_op | source)
XLA Modules:
  0.0 252.5 jit_solution(8515064198850389125)
XLA Ops:
  0.6 9.5 %pool.1 = (bf16[8,640,128]{2,1,0:T(8,128)(2,1)}, f32[256,128]{1,0:T(8,128)}) custom-call(bf16[32768,128]{1,0:T(8,128)(2,1)} %bitcast.10, s32[16,256]{1,0:T(8,128)} %bitcast.15, bf16[16,128]{1,0:T(8,128)(2,1)} %q_ref.1, bf16[64,256]{1,0:T(8,128)(2,1)} %bitcast.14), custom_call_target="tpu_custom_call" | custom-call | tf_op jit(solution)/shard_map/pool/pallas_call | solution.py:104
  10.2 5.5 %all-to-all-start = ((bf16[8,640,128]{2,1,0:T(8,128)(2,1)}), bf16[8,640,128]{2,1,0:T(8,128)(2,1)S(1)}, u32[]{:S(2)}, u32[]{:S(2)}) async-start(bf16[8,640,128]{2,1,0:T(8,128)(2,1)} %get-tuple-element.39), calls=%async_computation | async-start | bytes 2621440 | tf_op jit(solution)/shard_map/all_to_all | solution.py:551
  15.7 0.6 pad.8.projt_ref
  16.3 17.9 %all-to-all-done.recv_ref.refs_8_ = bf16[8,640,128]{2,1,0:T(8,128)(2,1)S(1)} async-done(((bf16[8,640,128]{2,1,0:T(8,128)(2,1)}), bf16[8,640,128]{2,1,0:T(8,128)(2,1)S(1)}, u32[]{:S(2)}, u32[]{:S(2)}) %all-to-all-start) | async-done | bytes 1310752 | tf_op jit(solution)/shard_map/all_to_all | solution.py:551
  34.2 1.1 copy-done.1
  35.3 5.5 %fm_forward.1 = (bf16[8,32,1024]{2,1,0:T(8,128)(2,1)}, f32[32,1024]{1,0:T(8,128)}, f32[32,128]{1,0:T(8,128)}, f32[256,128]{1,0:T(8,128)}, bf16[512,256]{1,0:T(8,128)(2,1)}) custom-call(bf16[8,640,128]{2,1,0:T(8,128)(2,1)} %copy-done.1, bf16[16,128]{1,0:T(8,128)(2,1)} %pad.8.projt_ref), custom_call_target="tpu_custom_call" | custom-call | tf_op jit(solution)/shard_map/fm_forward/pallas_call | solution.py:171
  40.8 3.5 %all-to-all-start.1 = ((bf16[8,32,1024]{2,1,0:T(8,128)(2,1)}), bf16[8,32,1024]{2,1,0:T(8,128)(2,1)S(1)}, u32[]{:S(2)}, u32[]{:S(2)}) async-start(bf16[8,32,1024]{2,1,0:T(8,128)(2,1)} %get-tuple-element.40), calls=%async_computation.1 | async-start | bytes 1048576 | tf_op jit(solution)/shard_map/all_to_all | solution.py:551
  44.3 9.4 %all-to-all-done.1 = bf16[8,32,1024]{2,1,0:T(8,128)(2,1)S(1)} async-done(((bf16[8,32,1024]{2,1,0:T(8,128)(2,1)}), bf16[8,32,1024]{2,1,0:T(8,128)(2,1)S(1)}, u32[]{:S(2)}, u32[]{:S(2)}) %all-to-all-start.1) | async-done | bytes 524320 | tf_op jit(solution)/shard_map/all_to_all | solution.py:551
  53.8 0.8 copy-done.2
  54.6 7.2 %layer_first.1 = (bf16[8,192,1024]{2,1,0:T(8,128)(2,1)}, bf16[256,1024]{1,0:T(8,128)(2,1)}, bf16[256,1024]{1,0:T(8,128)(2,1)}) custom-call(s32[1]{0:T(128)} %bitcast.7.half_ref, bf16[256,1024]{1,0:T(8,128)(2,1)} %bitcast.12, bf16[512,256]{1,0:T(8,128)(2,1)} %get-tuple-element.41.cott_hbm, bf16[1024,2048]{1,0:T(8,128)(2,1)} %up_hbm.3, bf16[2048,512]{1,0:T(8,128)(2,1)} %down_hbm.3), custom_call_target="tpu_custom_call" | custom-call | tf_op jit(solution)/shard_map/layer_first/pallas_call | solution.py:338
  61.8 0.3 collective-permute-start.7
  62.1 0.6 pad_add_fusion.half_ref
  62.7 9.9 %layer_second.1 = (bf16[8,192,1024]{2,1,0:T(8,128)(2,1)}, bf16[48,1024]{1,0:T(8,128)(2,1)}, bf16[48,1024]{1,0:T(8,128)(2,1)}, bf16[48,1024]{1,0:T(8,128)(2,1)}, ...) custom-call(s32[2]{0:T(128)} %pad_add_fusion.half_ref, ...), custom_call_target="tpu_custom_call" | custom-call | tf_op jit(solution)/shard_map/layer_second/pallas_call | solution.py:338
  72.6 0.0 collective-permute-done.7
  72.6 3.4 %add_convert_fusion = bf16[8,192,1024]{2,1,0:T(8,128)(2,1)S(1)} fusion(bf16[8,192,1024]{2,1,0:T(8,128)(2,1)S(1)} %collective-permute-done.7, bf16[8,192,1024]{2,1,0:T(8,128)(2,1)} %get-tuple-element.56), kind=kLoop, calls=%fused_computation | loop fusion | flops 6291456 | bytes 9437184 | tf_op jit(solution)/shard_map/convert_element_type | solution.py:573
  76.0 47.4 %all_to_all.20 = bf16[8,192,1024]{2,1,0:T(8,128)(2,1)S(1)} all-to-all(bf16[8,192,1024]{2,1,0:T(8,128)(2,1)S(1)} %add_convert_fusion), channel_id=1, replica_groups={{0,16,32,48,64,80,96,112},{8,24,40,56,72,88,104,120},{1,17,33,49,65,81,..., dimensions={0} | all-to-all | bytes 6291456 | tf_op jit(solution)/shard_map/all_to_all | solution.py:526
  123.5 0.6 reduce_sum.12
  124.1 0.4 broadcast_in_dim.18
  124.5 42.7 %all_to_all.21.stack_hbm = bf16[8,192,1024]{2,1,0:T(8,128)(2,1)S(1)} all-to-all(bf16[8,192,1024]{2,1,0:T(8,128)(2,1)S(1)} %broadcast_in_dim.18), channel_id=1, replica_groups={{0,16,32,48,64,80,96,112},{8,24,40,56,72,88,104,120},{1,17,33,49,65,81,..., dimensions={0} | all-to-all | bytes 6291456 | tf_op jit(solution)/shard_map/all_to_all | solution.py:526
  167.2 0.7 collective-permute-start
  167.9 0.6 collective-permute-start.1
  168.5 2.3 collective-permute-start.2
  170.8 0.9 collective-permute-start.3
  171.6 1.3 collective-permute-done.refs_1_
  172.9 1.4 collective-permute-start.4
  174.4 1.2 collective-permute-done.1.refs_2_
  175.6 1.1 collective-permute-start.5
  176.6 4.2 %collective-permute-start.6 = (bf16[48,1024]{1,0:T(8,128)(2,1)}, bf16[48,1024]{1,0:T(8,128)(2,1)}, u32[]{:S(2)}, u32[]{:S(2)}) collective-permute-start(bf16[48,1024]{1,0:T(8,128)(2,1)} %get-tuple-element.51), channel_id=1, source_target_pairs={{0,7},{1,6},{2,5},{3,4},{4,3},{5,2},{6,1},{7,0},{8,15},{9,14},{10,... | collective-permute-start | bytes 294920 | tf_op jit(solution)/shard_map/ppermute | solution.py:536
  180.8 0.1 copy.16
  180.9 0.6 pad.9.refs_9_
  181.6 0.0 collective-permute-done.3.refs_4_
  181.6 0.0 collective-permute-done.4.refs_5_
  181.6 2.4 collective-permute-done.5.refs_6_
  184.0 0.0 collective-permute-done.6.refs_7_
  184.0 6.6 %fm_backward.1 = (bf16[512,128]{1,0:T(8,128)(2,1)}, bf16[512,128]{1,0:T(8,128)(2,1)}, bf16[512,128]{1,0:T(8,128)(2,1)}, bf16[512,128]{1,0:T(8,128)(2,1)}, bf16[5...) custom-call(s32[1]{0:T(128)} %bitcast.rank_ref, ...), custom_call_target="tpu_custom_call" | custom-call | tf_op jit(solution)/shard_map/fm_backward/pallas_call | solution.py:403
  190.6 1.4 collective-permute-start.9
  192.0 2.2 collective-permute-start.11
  194.1 2.4 collective-permute-start.12
  196.5 0.1 collective-permute-done.9.refs_1_
  196.6 2.9 %collective-permute-start.13 = (bf16[512,128]{1,0:T(8,128)(2,1)}, bf16[512,128]{1,0:T(8,128)(2,1)}, u32[]{:S(2)}, u32[]{:S(2)}) collective-permute-start(bf16[512,128]{1,0:T(8,128)(2,1)} %get-tuple-element.67), channel_id=1, source_target_pairs={{0,5},{1,4},{2,7},{3,6},{4,1},{5,0},{6,3},{7,2},{8,13},{9,12},{10,... | collective-permute-start | bytes 393224 | tf_op jit(solution)/shard_map/ppermute | solution.py:536
  199.4 2.3 collective-permute-done.10.refs_2_
  201.7 3.7 %collective-permute-start.14 = (bf16[512,128]{1,0:T(8,128)(2,1)}, bf16[512,128]{1,0:T(8,128)(2,1)}, u32[]{:S(2)}, u32[]{:S(2)}) collective-permute-start(bf16[512,128]{1,0:T(8,128)(2,1)} %get-tuple-element.68), channel_id=1, source_target_pairs={{0,6},{1,7},{2,4},{3,5},{4,2},{5,3},{6,0},{7,1},{8,14},{9,15},{10,... | collective-permute-start | bytes 393224 | tf_op jit(solution)/shard_map/ppermute | solution.py:536
  205.4 1.3 collective-permute-start.15
  206.7 0.5 iota_xor_fusion.idx_ref
  207.2 0.0 collective-permute-done.12.refs_4_
  207.2 2.2 collective-permute-done.14.refs_6_
  209.4 3.4 %collective-permute-done.15.refs_7_ = bf16[512,128]{1,0:T(8,128)(2,1)} collective-permute-done((bf16[512,128]{1,0:T(8,128)(2,1)}, bf16[512,128]{1,0:T(8,128)(2,1)}, u32[]{:S(2)}, u32[]{:S(2)}) %collective-permute-start.15) | collective-permute-done | bytes 131104 | tf_op jit(solution)/shard_map/ppermute | solution.py:536
  212.8 12.2 %query_gradient.1 = (f32[16,128]{1,0:T(8,128)}, bf16[4096,128]{1,0:T(8,128)(2,1)}) custom-call(s32[8]{0:T(128)} %iota_xor_fusion.idx_ref, bf16[32768,128]{1,0:T(8,128)(2,1)} %bitcast.11, bf16[512,128]{1,0:T(8,128)(2,1)} %get-tuple-element.62.refs_0_, bf16[512,128]{1,0:T(8,128)(2,1)} %copy-done.3, bf16[512,128]{1,0:T(8,128)(2,1)} %copy-done.4, ...), custom_call_target="tpu_custom_call" | custom-call | tf_op jit(solution)/shard_map/query_gradient/pallas_call | solution.py:455
  225.0 0.1 collective-permute-start.16
  225.1 1.4 collective-permute-done.16
  226.5 0.7 add_convert_fusion.1
  227.2 0.3 collective-permute-start.23
  227.4 4.4 %collective-permute-start.22 = (bf16[16,128]{1,0:T(8,128)(2,1)S(1)}, bf16[16,128]{1,0:T(8,128)(2,1)S(1)}, u32[]{:S(2)}, u32[]{:S(2)}) collective-permute-start(bf16[16,128]{1,0:T(8,128)(2,1)S(1)} %add_convert_fusion.1), channel_id=1, source_target_pairs={{0,96},{8,104},{16,112},{24,120},{32,64},{40,72},{48,80},{56,88},{... | collective-permute-start | bytes 12296 | tf_op jit(solution)/shard_map/ppermute | solution.py:547
  231.9 0.5 collective-permute-start.21
  232.4 2.5 %collective-permute-start.20 = (bf16[16,128]{1,0:T(8,128)(2,1)S(1)}, bf16[16,128]{1,0:T(8,128)(2,1)S(1)}, u32[]{:S(2)}, u32[]{:S(2)}) collective-permute-start(bf16[16,128]{1,0:T(8,128)(2,1)S(1)} %add_convert_fusion.1), channel_id=1, source_target_pairs={{0,64},{8,72},{16,80},{24,88},{32,96},{40,104},{48,112},{56,120},{... | collective-permute-start | bytes 12296 | tf_op jit(solution)/shard_map/ppermute | solution.py:547
  234.9 3.2 %collective-permute-start.19 = (bf16[16,128]{1,0:T(8,128)(2,1)S(1)}, bf16[16,128]{1,0:T(8,128)(2,1)S(1)}, u32[]{:S(2)}, u32[]{:S(2)}) collective-permute-start(bf16[16,128]{1,0:T(8,128)(2,1)S(1)} %add_convert_fusion.1), channel_id=1, source_target_pairs={{0,48},{8,56},{16,0},{24,8},{32,16},{40,24},{48,32},{56,40},{64,11... | collective-permute-start | bytes 12296 | tf_op jit(solution)/shard_map/ppermute | solution.py:547
  238.1 0.9 collective-permute-start.18
  238.9 0.1 collective-permute-done.21
  239.1 1.1 collective-permute-start.17
  240.2 3.0 %collective-permute-done.18 = bf16[16,128]{1,0:T(8,128)(2,1)S(1)} collective-permute-done((bf16[16,128]{1,0:T(8,128)(2,1)S(1)}, bf16[16,128]{1,0:T(8,128)(2,1)S(1)}, u32[]{:S(2)}, u32[]{:S(2)}) %collective-permute-start.18) | collective-permute-done | bytes 4128 | tf_op jit(solution)/shard_map/ppermute | solution.py:547
  243.2 0.7 collective-permute-done.17
  243.9 0.6 convert_add_fusion
  244.5 3.9 %own_half.1 = (f32[1024,2048]{1,0:T(8,128)}, f32[2048,512]{1,0:T(8,128)}) custom-call(s32[1]{0:T(128)} %bitcast.1.half_ref, bf16[8,192,1024]{2,1,0:T(8,128)(2,1)} %copy-done), custom_call_target="tpu_custom_call" | custom-call | tf_op jit(solution)/shard_map/own_half/pallas_call | solution.py:506
  248.4 3.9 %other_half.1 = (f32[1024,2048]{1,0:T(8,128)}, f32[2048,512]{1,0:T(8,128)}) custom-call(s32[1]{0:T(128)} %bitcast.7.half_ref, bf16[8,192,1024]{2,1,0:T(8,128)(2,1)} %collective-permute-done.8.stack_hbm, f32[1024,2048]{1,0:T(8,128)} %get-tuple-element.58.refs_0_, f32[2048,512]{1,0:T(8,128)} %get-tuple-element.59.refs_1_), custom_call_target="tpu_custom_call", output_to_operand_aliasing={{0}: (2, {}), {1}: (3, {})} | custom-call | tf_op jit(solution)/shard_map/other_half/pallas_call | solution.py:506
  (35 shorter events, 0.1 us)
Async XLA Ops:
  0.6 15.0 %copy-start.9 = (bf16[128,8]{0,1:T(8,128)(2,1)S(1)}, bf16[128,8]{0,1:T(8,128)(2,1)}, u32[]{:S(2)}) copy-start(bf16[128,8]{0,1:T(8,128)(2,1)} %param.10) | copy-start | bytes 6148
  10.2 24.1 %all-to-all-start = ((bf16[8,640,128]{2,1,0:T(8,128)(2,1)}), bf16[8,640,128]{2,1,0:T(8,128)(2,1)S(1)}, u32[]{:S(2)}, u32[]{:S(2)}) async-start(bf16[8,640,128]{2,1,0:T(8,128)(2,1)} %get-tuple-element.39), calls=%async_computation | async-start | bytes 2621440 | tf_op jit(solution)/shard_map/all_to_all | solution.py:551
  34.2 1.1 copy-start.1
  40.8 13.0 %all-to-all-start.1 = ((bf16[8,32,1024]{2,1,0:T(8,128)(2,1)}), bf16[8,32,1024]{2,1,0:T(8,128)(2,1)S(1)}, u32[]{:S(2)}, u32[]{:S(2)}) async-start(bf16[8,32,1024]{2,1,0:T(8,128)(2,1)} %get-tuple-element.40), calls=%async_computation.1 | async-start | bytes 1048576 | tf_op jit(solution)/shard_map/all_to_all | solution.py:551
  53.8 0.8 copy-start.2
  61.8 10.8 %collective-permute-start.7 = (bf16[8,192,1024]{2,1,0:T(8,128)(2,1)}, bf16[8,192,1024]{2,1,0:T(8,128)(2,1)S(1)}, u32[]{:S(2)}, u32[]{:S(2)}) collective-permute-start(bf16[8,192,1024]{2,1,0:T(8,128)(2,1)} %get-tuple-element.57), channel_id=1, source_target_pairs={{0,8},{8,0},{16,24},{24,16},{32,40},{40,32},{48,56},{56,48},{64,72... | collective-permute-start | bytes 9437192 | tf_op jit(solution)/shard_map/ppermute | solution.py:530
  124.5 42.7 %copy-start.12 = (bf16[48,1024]{1,0:T(8,128)(2,1)S(1)}, bf16[48,1024]{1,0:T(8,128)(2,1)}, u32[]{:S(2)}) copy-start(bf16[48,1024]{1,0:T(8,128)(2,1)} %get-tuple-element.45) | copy-start | bytes 294916
  124.5 43.4 %copy-start.11 = (bf16[48,1024]{1,0:T(8,128)(2,1)S(1)}, bf16[48,1024]{1,0:T(8,128)(2,1)}, u32[]{:S(2)}) copy-start(bf16[48,1024]{1,0:T(8,128)(2,1)} %get-tuple-element.46) | copy-start | bytes 294916
  124.5 44.0 %copy-start.10 = (bf16[48,1024]{1,0:T(8,128)(2,1)S(1)}, bf16[48,1024]{1,0:T(8,128)(2,1)}, u32[]{:S(2)}) copy-start(bf16[48,1024]{1,0:T(8,128)(2,1)} %get-tuple-element.47) | copy-start | bytes 294916
  167.2 57.8 %copy-start = (bf16[8,192,1024]{2,1,0:T(8,128)(2,1)}, bf16[8,192,1024]{2,1,0:T(8,128)(2,1)S(1)}, u32[]{:S(2)}) copy-start(bf16[8,192,1024]{2,1,0:T(8,128)(2,1)S(1)} %all_to_all.21.stack_hbm) | copy-start | bytes 9437188
  167.2 81.2 %collective-permute-start.8 = (bf16[8,192,1024]{2,1,0:T(8,128)(2,1)S(1)}, bf16[8,192,1024]{2,1,0:T(8,128)(2,1)}, u32[]{:S(2)}, u32[]{:S(2)}) collective-permute-start(bf16[8,192,1024]{2,1,0:T(8,128)(2,1)S(1)} %all_to_all.21.stack_hbm), channel_id=1, source_target_pairs={{0,8},{8,0},{16,24},{24,16},{32,40},{40,32},{48,56},{56,48},{64,72... | collective-permute-start | bytes 9437192 | tf_op jit(solution)/shard_map/ppermute | solution.py:530
  167.2 5.7 %collective-permute-start = (bf16[48,1024]{1,0:T(8,128)(2,1)S(1)}, bf16[48,1024]{1,0:T(8,128)(2,1)S(1)}, u32[]{:S(2)}, u32[]{:S(2)}) collective-permute-start(bf16[48,1024]{1,0:T(8,128)(2,1)S(1)} %copy-done.12), channel_id=1, source_target_pairs={{0,1},{1,0},{2,3},{3,2},{4,5},{5,4},{6,7},{7,6},{8,9},{9,8},{10,11... | collective-permute-start | bytes 294920 | tf_op jit(solution)/shard_map/ppermute | solution.py:536
  167.9 7.6 %collective-permute-start.1 = (bf16[48,1024]{1,0:T(8,128)(2,1)S(1)}, bf16[48,1024]{1,0:T(8,128)(2,1)S(1)}, u32[]{:S(2)}, u32[]{:S(2)}) collective-permute-start(bf16[48,1024]{1,0:T(8,128)(2,1)S(1)} %copy-done.11), channel_id=1, source_target_pairs={{0,2},{1,3},{2,0},{3,1},{4,6},{5,7},{6,4},{7,5},{8,10},{9,11},{10,... | collective-permute-start | bytes 294920 | tf_op jit(solution)/shard_map/ppermute | solution.py:536
  168.5 8.1 %collective-permute-start.2 = (bf16[48,1024]{1,0:T(8,128)(2,1)S(1)}, bf16[48,1024]{1,0:T(8,128)(2,1)S(1)}, u32[]{:S(2)}, u32[]{:S(2)}) collective-permute-start(bf16[48,1024]{1,0:T(8,128)(2,1)S(1)} %copy-done.10), channel_id=1, source_target_pairs={{0,3},{1,2},{2,1},{3,0},{4,7},{5,6},{6,5},{7,4},{8,11},{9,10},{10,... | collective-permute-start | bytes 294920 | tf_op jit(solution)/shard_map/ppermute | solution.py:536
  170.8 10.8 %collective-permute-start.3 = (bf16[48,1024]{1,0:T(8,128)(2,1)}, bf16[48,1024]{1,0:T(8,128)(2,1)}, u32[]{:S(2)}, u32[]{:S(2)}) collective-permute-start(bf16[48,1024]{1,0:T(8,128)(2,1)} %get-tuple-element.48), channel_id=1, source_target_pairs={{0,4},{1,5},{2,6},{3,7},{4,0},{5,1},{6,2},{7,3},{8,12},{9,13},{10,... | collective-permute-start | bytes 294920 | tf_op jit(solution)/shard_map/ppermute | solution.py:536
  172.9 11.1 %copy-start.6 = (bf16[48,1024]{1,0:T(8,128)(2,1)}, bf16[48,1024]{1,0:T(8,128)(2,1)S(1)}, u32[]{:S(2)}) copy-start(bf16[48,1024]{1,0:T(8,128)(2,1)S(1)} %collective-permute-done.refs_1_) | copy-start | bytes 294916
  172.9 8.6 %collective-permute-start.4 = (bf16[48,1024]{1,0:T(8,128)(2,1)}, bf16[48,1024]{1,0:T(8,128)(2,1)}, u32[]{:S(2)}, u32[]{:S(2)}) collective-permute-start(bf16[48,1024]{1,0:T(8,128)(2,1)} %get-tuple-element.49), channel_id=1, source_target_pairs={{0,5},{1,4},{2,7},{3,6},{4,1},{5,0},{6,3},{7,2},{8,13},{9,12},{10,... | collective-permute-start | bytes 294920 | tf_op jit(solution)/shard_map/ppermute | solution.py:536
  175.5 8.5 %copy-start.7 = (bf16[48,1024]{1,0:T(8,128)(2,1)}, bf16[48,1024]{1,0:T(8,128)(2,1)S(1)}, u32[]{:S(2)}) copy-start(bf16[48,1024]{1,0:T(8,128)(2,1)S(1)} %collective-permute-done.1.refs_2_) | copy-start | bytes 294916
  175.6 8.5 %collective-permute-start.5 = (bf16[48,1024]{1,0:T(8,128)(2,1)}, bf16[48,1024]{1,0:T(8,128)(2,1)}, u32[]{:S(2)}, u32[]{:S(2)}) collective-permute-start(bf16[48,1024]{1,0:T(8,128)(2,1)} %get-tuple-element.50), channel_id=1, source_target_pairs={{0,6},{1,7},{2,4},{3,5},{4,2},{5,3},{6,0},{7,1},{8,14},{9,15},{10,... | collective-permute-start | bytes 294920 | tf_op jit(solution)/shard_map/ppermute | solution.py:536
  176.6 7.4 %copy-start.8 = (bf16[48,1024]{1,0:T(8,128)(2,1)}, bf16[48,1024]{1,0:T(8,128)(2,1)S(1)}, u32[]{:S(2)}) copy-start(bf16[48,1024]{1,0:T(8,128)(2,1)S(1)} %collective-permute-done.2.refs_3_) | copy-start | bytes 294916
  176.6 7.4 %collective-permute-start.6 = (bf16[48,1024]{1,0:T(8,128)(2,1)}, bf16[48,1024]{1,0:T(8,128)(2,1)}, u32[]{:S(2)}, u32[]{:S(2)}) collective-permute-start(bf16[48,1024]{1,0:T(8,128)(2,1)} %get-tuple-element.51), channel_id=1, source_target_pairs={{0,7},{1,6},{2,5},{3,4},{4,3},{5,2},{6,1},{7,0},{8,15},{9,14},{10,... | collective-permute-start | bytes 294920 | tf_op jit(solution)/shard_map/ppermute | solution.py:536
  190.6 6.0 %collective-permute-start.9 = (bf16[512,128]{1,0:T(8,128)(2,1)}, bf16[512,128]{1,0:T(8,128)(2,1)S(1)}, u32[]{:S(2)}, u32[]{:S(2)}) collective-permute-start(bf16[512,128]{1,0:T(8,128)(2,1)} %get-tuple-element.63), channel_id=1, source_target_pairs={{0,1},{1,0},{2,3},{3,2},{4,5},{5,4},{6,7},{7,6},{8,9},{9,8},{10,11... | collective-permute-start | bytes 393224 | tf_op jit(solution)/shard_map/ppermute | solution.py:536
  192.0 9.8 %collective-permute-start.10 = (bf16[512,128]{1,0:T(8,128)(2,1)}, bf16[512,128]{1,0:T(8,128)(2,1)S(1)}, u32[]{:S(2)}, u32[]{:S(2)}) collective-permute-start(bf16[512,128]{1,0:T(8,128)(2,1)} %get-tuple-element.64), channel_id=1, source_target_pairs={{0,2},{1,3},{2,0},{3,1},{4,6},{5,7},{6,4},{7,5},{8,10},{9,11},{10,... | collective-permute-start | bytes 393224 | tf_op jit(solution)/shard_map/ppermute | solution.py:536
  192.0 13.5 %collective-permute-start.11 = (bf16[512,128]{1,0:T(8,128)(2,1)}, bf16[512,128]{1,0:T(8,128)(2,1)S(1)}, u32[]{:S(2)}, u32[]{:S(2)}) collective-permute-start(bf16[512,128]{1,0:T(8,128)(2,1)} %get-tuple-element.65), channel_id=1, source_target_pairs={{0,3},{1,2},{2,1},{3,0},{4,7},{5,6},{6,5},{7,4},{8,11},{9,10},{10,... | collective-permute-start | bytes 393224 | tf_op jit(solution)/shard_map/ppermute | solution.py:536
  194.1 13.1 %collective-permute-start.12 = (bf16[512,128]{1,0:T(8,128)(2,1)}, bf16[512,128]{1,0:T(8,128)(2,1)}, u32[]{:S(2)}, u32[]{:S(2)}) collective-permute-start(bf16[512,128]{1,0:T(8,128)(2,1)} %get-tuple-element.66), channel_id=1, source_target_pairs={{0,4},{1,5},{2,6},{3,7},{4,0},{5,1},{6,2},{7,3},{8,12},{9,13},{10,... | collective-permute-start | bytes 393224 | tf_op jit(solution)/shard_map/ppermute | solution.py:536
  196.6 16.3 %copy-start.3 = (bf16[512,128]{1,0:T(8,128)(2,1)}, bf16[512,128]{1,0:T(8,128)(2,1)S(1)}, u32[]{:S(2)}) copy-start(bf16[512,128]{1,0:T(8,128)(2,1)S(1)} %collective-permute-done.9.refs_1_) | copy-start | bytes 393220
  196.6 10.7 %collective-permute-start.13 = (bf16[512,128]{1,0:T(8,128)(2,1)}, bf16[512,128]{1,0:T(8,128)(2,1)}, u32[]{:S(2)}, u32[]{:S(2)}) collective-permute-start(bf16[512,128]{1,0:T(8,128)(2,1)} %get-tuple-element.67), channel_id=1, source_target_pairs={{0,5},{1,4},{2,7},{3,6},{4,1},{5,0},{6,3},{7,2},{8,13},{9,12},{10,... | collective-permute-start | bytes 393224 | tf_op jit(solution)/shard_map/ppermute | solution.py:536
  201.7 11.1 %copy-start.4 = (bf16[512,128]{1,0:T(8,128)(2,1)}, bf16[512,128]{1,0:T(8,128)(2,1)S(1)}, u32[]{:S(2)}) copy-start(bf16[512,128]{1,0:T(8,128)(2,1)S(1)} %collective-permute-done.10.refs_2_) | copy-start | bytes 393220
  201.7 7.7 %collective-permute-start.14 = (bf16[512,128]{1,0:T(8,128)(2,1)}, bf16[512,128]{1,0:T(8,128)(2,1)}, u32[]{:S(2)}, u32[]{:S(2)}) collective-permute-start(bf16[512,128]{1,0:T(8,128)(2,1)} %get-tuple-element.68), channel_id=1, source_target_pairs={{0,6},{1,7},{2,4},{3,5},{4,2},{5,3},{6,0},{7,1},{8,14},{9,15},{10,... | collective-permute-start | bytes 393224 | tf_op jit(solution)/shard_map/ppermute | solution.py:536
  205.4 7.4 %copy-start.5 = (bf16[512,128]{1,0:T(8,128)(2,1)}, bf16[512,128]{1,0:T(8,128)(2,1)S(1)}, u32[]{:S(2)}) copy-start(bf16[512,128]{1,0:T(8,128)(2,1)S(1)} %collective-permute-done.11.refs_3_) | copy-start | bytes 393220
  205.4 7.4 %collective-permute-start.15 = (bf16[512,128]{1,0:T(8,128)(2,1)}, bf16[512,128]{1,0:T(8,128)(2,1)}, u32[]{:S(2)}, u32[]{:S(2)}) collective-permute-start(bf16[512,128]{1,0:T(8,128)(2,1)} %get-tuple-element.69), channel_id=1, source_target_pairs={{0,7},{1,6},{2,5},{3,4},{4,3},{5,2},{6,1},{7,0},{8,15},{9,14},{10,... | collective-permute-start | bytes 393224 | tf_op jit(solution)/shard_map/ppermute | solution.py:536
  225.0 1.5 collective-permute-start.16
  227.2 7.7 %collective-permute-start.23 = (bf16[16,128]{1,0:T(8,128)(2,1)S(1)}, bf16[16,128]{1,0:T(8,128)(2,1)S(1)}, u32[]{:S(2)}, u32[]{:S(2)}) collective-permute-start(bf16[16,128]{1,0:T(8,128)(2,1)S(1)} %add_convert_fusion.1), channel_id=1, source_target_pairs={{0,112},{8,120},{16,64},{24,72},{32,80},{40,88},{48,96},{56,104},{... | collective-permute-start | bytes 12296 | tf_op jit(solution)/shard_map/ppermute | solution.py:547
  227.4 10.6 %collective-permute-start.22 = (bf16[16,128]{1,0:T(8,128)(2,1)S(1)}, bf16[16,128]{1,0:T(8,128)(2,1)S(1)}, u32[]{:S(2)}, u32[]{:S(2)}) collective-permute-start(bf16[16,128]{1,0:T(8,128)(2,1)S(1)} %add_convert_fusion.1), channel_id=1, source_target_pairs={{0,96},{8,104},{16,112},{24,120},{32,64},{40,72},{48,80},{56,88},{... | collective-permute-start | bytes 12296 | tf_op jit(solution)/shard_map/ppermute | solution.py:547
  231.9 7.2 %collective-permute-start.21 = (bf16[16,128]{1,0:T(8,128)(2,1)S(1)}, bf16[16,128]{1,0:T(8,128)(2,1)S(1)}, u32[]{:S(2)}, u32[]{:S(2)}) collective-permute-start(bf16[16,128]{1,0:T(8,128)(2,1)S(1)} %add_convert_fusion.1), channel_id=1, source_target_pairs={{0,80},{8,88},{16,96},{24,104},{32,112},{40,120},{48,64},{56,72},{... | collective-permute-start | bytes 12296 | tf_op jit(solution)/shard_map/ppermute | solution.py:547
  232.4 7.8 %collective-permute-start.20 = (bf16[16,128]{1,0:T(8,128)(2,1)S(1)}, bf16[16,128]{1,0:T(8,128)(2,1)S(1)}, u32[]{:S(2)}, u32[]{:S(2)}) collective-permute-start(bf16[16,128]{1,0:T(8,128)(2,1)S(1)} %add_convert_fusion.1), channel_id=1, source_target_pairs={{0,64},{8,72},{16,80},{24,88},{32,96},{40,104},{48,112},{56,120},{... | collective-permute-start | bytes 12296 | tf_op jit(solution)/shard_map/ppermute | solution.py:547
  234.9 5.3 %collective-permute-start.19 = (bf16[16,128]{1,0:T(8,128)(2,1)S(1)}, bf16[16,128]{1,0:T(8,128)(2,1)S(1)}, u32[]{:S(2)}, u32[]{:S(2)}) collective-permute-start(bf16[16,128]{1,0:T(8,128)(2,1)S(1)} %add_convert_fusion.1), channel_id=1, source_target_pairs={{0,48},{8,56},{16,0},{24,8},{32,16},{40,24},{48,32},{56,40},{64,11... | collective-permute-start | bytes 12296 | tf_op jit(solution)/shard_map/ppermute | solution.py:547
  238.1 5.1 %collective-permute-start.18 = (bf16[16,128]{1,0:T(8,128)(2,1)S(1)}, bf16[16,128]{1,0:T(8,128)(2,1)S(1)}, u32[]{:S(2)}, u32[]{:S(2)}) collective-permute-start(bf16[16,128]{1,0:T(8,128)(2,1)S(1)} %add_convert_fusion.1), channel_id=1, source_target_pairs={{0,32},{8,40},{16,48},{24,56},{32,0},{40,8},{48,16},{56,24},{64,96... | collective-permute-start | bytes 12296 | tf_op jit(solution)/shard_map/ppermute | solution.py:547
  239.1 4.8 %collective-permute-start.17 = (bf16[16,128]{1,0:T(8,128)(2,1)S(1)}, bf16[16,128]{1,0:T(8,128)(2,1)S(1)}, u32[]{:S(2)}, u32[]{:S(2)}) collective-permute-start(bf16[16,128]{1,0:T(8,128)(2,1)S(1)} %add_convert_fusion.1), channel_id=1, source_target_pairs={{0,16},{8,24},{16,32},{24,40},{32,48},{40,56},{48,0},{56,8},{64,80... | collective-permute-start | bytes 12296 | tf_op jit(solution)/shard_map/ppermute | solution.py:547

commit v3 on v2

--- a/solution.py
+++ b/solution.py
@@ -46,7 +46,7 @@
     return x
 
 
-PARTS = 4
+PARTS = 2
 PER = MP // PARTS
 
 
@@ -65,34 +65,34 @@
     lens = dot(lent_ref[...].astype(f32).astype(bf16), spread, TN)
     live = (iota((U, E), 1) % L).astype(f32) < lens
     q = q_ref[...]
+    copies = []
     for g in range(PARTS):
         loads[g].wait()
         raw = dot(q, ev[g], NT)
+        first = g * PER * UB
+        here = slice(first, first + PER * UB)
         for u in range(PER * UB):
             block = jnp.where(mask, raw[:, u * E : (u + 1) * E], 0.0)
-            at = g * PER * UB + u
-            w[at : at + 1, :] = jnp.sum(block, axis=0, keepdims=True)
-    scores = w[...] * (1.0 / math.sqrt(E))
-    top = group_reduce(jnp.where(live, scores, -1e30), jnp.maximum)
-    ex = jnp.exp(jnp.where(live, scores - top, -1e30))
-    w[...] = ex / group_reduce(ex, jnp.add)
-    w_copy = pltpu.make_async_copy(w, w_hbm, w_sem)
-    w_copy.start()
-    stores = []
-    for p in range(MP):
-        for u in range(UB):
-            row = jnp.broadcast_to(w[p * UB + u : p * UB + u + 1, :], (FH, E))
-            mix = jnp.where(mask, row, 0.0).astype(bf16)
-            at = ((p % PER) * UB + u) * E
-            pooled = dot(mix, ev[p // PER, at : at + E, :])
-            send[p, u * FH : (u + 1) * FH, :] = pooled.astype(bf16)
-        send[p, UB * FH : UB * FH + 64, :] = cott_ref[:, 0:E]
-        send[p, UB * FH + 64 :, :] = cott_ref[:, E:]
-        stores.append(pltpu.make_async_copy(send.at[p], send_hbm.at[p], out_sem.at[p]))
-        stores[-1].start()
-    for store in stores:
-        store.wait()
-    w_copy.wait()
+            w[first + u : first + u + 1, :] = jnp.sum(block, axis=0, keepdims=True)
+        scores = w[here, :] * (1.0 / math.sqrt(E))
+        top = group_reduce(jnp.where(live[here], scores, -1e30), jnp.maximum)
+        ex = jnp.exp(jnp.where(live[here], scores - top, -1e30))
+        w[here, :] = ex / group_reduce(ex, jnp.add)
+        for i in range(PER):
+            p = g * PER + i
+            for u in range(UB):
+                row = jnp.broadcast_to(w[p * UB + u : p * UB + u + 1, :], (FH, E))
+                weight = jnp.where(mask, row, 0.0).astype(bf16)
+                at = (i * UB + u) * E
+                pooled = dot(weight, ev[g, at : at + E, :])
+                send[p, u * FH : (u + 1) * FH, :] = pooled.astype(bf16)
+            send[p, UB * FH : UB * FH + 64, :] = cott_ref[:, 0:E]
+            send[p, UB * FH + 64 :, :] = cott_ref[:, E:]
+            copies.append(pltpu.make_async_copy(send.at[p], send_hbm.at[p], out_sem.at[p]))
+            copies[-1].start()
+    copies.append(pltpu.make_async_copy(w, w_hbm, w_sem))
+    copies[-1].start()
+    wait_all(copies)
 
 
 HBM = pl.BlockSpec(memory_space=pltpu.HBM)
@@ -136,40 +136,52 @@
     )
 
 
-def fm_kernel(recv_ref, projt_ref, send_ref, normed_ref, inv_ref, mix_ref, cot_ref, scr):
+def fm_kernel(recv_ref, projt_ref, *refs):
+    outs, (rows, normed, inv_v, mix_v, cot, scr, row_sem, sem) = refs[:5], refs[5:]
     mask = flat_mask()
     projt = projt_ref[...]
+    at = UB * FH
+    for j in range(MP):
+        cot[j * 64 : (j + 1) * 64, 0:E] = recv_ref[j, at : at + 64, :]
+        cot[j * 64 : (j + 1) * 64, E:] = recv_ref[j, at + 64 :, :]
+    copies = [
+        pltpu.make_async_copy(v, o, sem.at[i])
+        for i, (v, o) in enumerate(zip((normed, inv_v, mix_v, cot), outs[1:]))
+    ]
+    copies[3].start()
 
     def step(u, carry):
         p = user_rows(recv_ref, u)
         mix = dot(projt, p)[0:R].astype(bf16).astype(f32)
         full = jnp.where(mask, dot(p, tile_ranks(mix), NT), 0.0)
         at = pl.multiple_of(u * R, R)
-        mix_ref[pl.ds(at, R), :] = mix
+        mix_v[pl.ds(at, R), :] = mix
         scr[pl.ds(at, R), :] = jnp.sum(full.reshape(MP, FH, E), axis=1)
         return carry
 
-    lax.fori_loop(0, UB, step, 0, unroll=16)
+    lax.fori_loop(0, UB, step, 0, unroll=32)
+    copies[2].start()
     total = jnp.zeros((UB, 1), f32)
     for j in range(MP):
         x = scr[pl.ds(j, UB, stride=R), :]
         total = total + jnp.sum(x * x, axis=1, keepdims=True)
     inv = lax.rsqrt(total * (1.0 / (E * R)) + norm_eps)
-    inv_ref[...] = jnp.broadcast_to(inv, (UB, E))
+    inv_v[...] = jnp.broadcast_to(inv, (UB, E))
     for j in range(MP):
         x = scr[pl.ds(j, UB, stride=R), :] * inv
-        normed_ref[:, j * E : (j + 1) * E] = x
-        for p in range(MP):
-            send_ref[p, :, j * E : (j + 1) * E] = x.astype(bf16)
-    at = UB * FH
-    for j in range(MP):
-        cot_ref[j * 64 : (j + 1) * 64, 0:E] = recv_ref[j, at : at + 64, :]
-        cot_ref[j * 64 : (j + 1) * 64, E:] = recv_ref[j, at + 64 :, :]
+        normed[:, j * E : (j + 1) * E] = x
+        rows[:, j * E : (j + 1) * E] = x.astype(bf16)
+    copies += [pltpu.make_async_copy(rows, outs[0].at[p], row_sem.at[p]) for p in range(MP)]
+    start_all(copies[4:])
+    start_all(copies[:2])
+    wait_all(copies)
 
 
 def fm_call(recv, projt):
     return pl.pallas_call(
         fm_kernel,
+        in_specs=[VMEM, VMEM],
+        out_specs=[HBM] * 5,
         out_shape=[
             jax.ShapeDtypeStruct((MP, UB, E * R), bf16),
             jax.ShapeDtypeStruct((UB, E * R), f32),
@@ -177,7 +189,16 @@
             jax.ShapeDtypeStruct((UB * R, E), f32),
             jax.ShapeDtypeStruct((512, U), bf16),
         ],
-        scratch_shapes=[pltpu.VMEM((UB * R, E), f32)],
+        scratch_shapes=[
+            pltpu.VMEM((UB, E * R), bf16),
+            pltpu.VMEM((UB, E * R), f32),
+            pltpu.VMEM((UB, E), f32),
+            pltpu.VMEM((UB * R, E), f32),
+            pltpu.VMEM((512, U), bf16),
+            pltpu.VMEM((UB * R, E), f32),
+            pltpu.SemaphoreType.DMA((MP,)),
+            pltpu.SemaphoreType.DMA((4,)),
+        ],
         name="fm_forward",
     )(recv, projt)
 
@@ -187,18 +208,13 @@
 HALF = HB * STEPS
 
 
-def weight_loads(half, up_hbm, down_hbm, up, down, sem):
-    loads = []
-    for k in range(STEPS):
-        at = pl.multiple_of(half * HALF + k * HB, HB)
-        here = pl.ds(k * HB, HB)
-        loads.append(
-            (
-                pltpu.make_async_copy(up_hbm.at[:, pl.ds(at, HB)], up.at[:, here], sem.at[0, k]),
-                pltpu.make_async_copy(down_hbm.at[pl.ds(at, HB)], down.at[here], sem.at[1, k]),
-            )
-        )
-    return loads
+def weight_loads(half, up_hbm, down_hbm, up, down, sem, k):
+    at = pl.multiple_of(half * HALF + k * HB, HB)
+    here = pl.ds(pl.multiple_of(k * HB, HB), HB)
+    return [
+        pltpu.make_async_copy(up_hbm.at[:, pl.ds(at, HB)], up.at[:, here], sem.at[0, k]),
+        pltpu.make_async_copy(down_hbm.at[pl.ds(at, HB)], down.at[here], sem.at[1, k]),
+    ]
 
 
 def start_all(copies):
@@ -211,91 +227,94 @@
         copy.wait()
 
 
-def layer_half(loads, n, nt, cot, up, down, act, dh, g, g_hbm, sem):
-    stores = []
-    for k in range(STEPS):
-        wait_all(loads[k])
-        cols = slice(k * HB, (k + 1) * HB)
-        hidden = dot(n, up[:, cols])
-        d_act = dot(cot, down[cols, :], NT)
+def gradient_stores(g, g_hbm, sem, k):
+    here = pl.ds(pl.multiple_of(k * HB, HB), HB)
+    pair = pl.ds(2 * k, 2)
+    low = pl.ds(E, 64)
+    return [
+        pltpu.make_async_copy(
+            g.at[:, pl.ds(0, E), here], g_hbm.at[:, pl.ds(0, E), here], sem.at[0, k]
+        ),
+        pltpu.make_async_copy(g.at[pair, low], g_hbm.at[pair, low], sem.at[1, k]),
+    ]
+
+
+def layer_half(loads, stores, n, nt, cot, up, down, act, dh, g):
+    def block(k, carry):
+        wait_all(loads(k))
+        cols = pl.ds(pl.multiple_of(k * HB, HB), HB)
+        hidden = dot(n[...], up[:, cols])
+        d_act = dot(cot[...], down[cols, :], NT)
         s = 1.0 / (1.0 + jnp.exp(-hidden))
         act_k = (hidden * s).astype(bf16)
         dh_k = (d_act * s * (1.0 + hidden * (1.0 - s))).astype(bf16)
         act[:, cols] = act_k
         dh[:, cols] = dh_k
-        g[:, 0:E, cols] = dot(nt, dh_k).astype(bf16).reshape(MP, E, HB)
-        g_down = dot(act_k, cot, TN).astype(bf16)
+        g[:, 0:E, cols] = dot(nt[...], dh_k).astype(bf16).reshape(MP, E, HB)
+        g_down = dot(act_k, cot[...], TN).astype(bf16)
         for t in range(2):
             for h in range(2):
                 at = t * 128 + h * 64
                 g[2 * k + t, E:, h * 512 : (h + 1) * 512] = g_down[at : at + 64, :]
-        here = pl.ds(k * HB, HB)
-        pair = pl.ds(2 * k, 2)
-        low = pl.ds(E, 64)
-        stores += [
-            pltpu.make_async_copy(
-                g.at[:, pl.ds(0, E), here], g_hbm.at[:, pl.ds(0, E), here], sem.at[0, k]
-            ),
-            pltpu.make_async_copy(g.at[pair, low], g_hbm.at[pair, low], sem.at[1, k]),
-        ]
-        start_all(stores[-2:])
-    return stores
+        start_all(stores(k))
+        return carry
+
+    lax.fori_loop(0, STEPS, block, 0)
 
 
 def layer_first(
-    half_ref, n_hbm, cott_hbm, up_hbm, down_hbm, g_hbm, act_hbm, dh_hbm,
-    n, nt, cott, up, down, act, dh, g, in_sem, w_sem, g_sem, out_sem,
+    half_ref, rank_ref, n_hbm, cott_hbm, up_hbm, down_hbm, g_hbm, act_hbm, dh_hbm,
+    n, nt, cott, cot, up, down, act, dh, g, in_sem, w_sem, g_sem, out_sem,
 ):
     first = [
         pltpu.make_async_copy(n_hbm, n, in_sem.at[0]),
         pltpu.make_async_copy(cott_hbm, cott, in_sem.at[1]),
     ]
-    loads = weight_loads(half_ref[0], up_hbm, down_hbm, up, down, w_sem)
+    loads = lambda k: weight_loads(half_ref[0], up_hbm, down_hbm, up, down, w_sem, k)
+    stores = lambda k: gradient_stores(g, g_hbm, g_sem, k)
     start_all(first)
-    for pair in loads:
-        start_all(pair)
+    for k in range(STEPS):
+        start_all(loads(k))
     wait_all(first)
-    rows = n[...]
-    nt[...] = rows.T
-    cot = cott[...].T
-    stores = layer_half(loads, rows, nt[...], cot, up, down, act, dh, g, g_hbm, g_sem)
+    nt[...] = n[...].T
+    cot[...] = cott[...].T
+    layer_half(loads, stores, n, nt, cot, up, down, act, dh, g)
     last = [
         pltpu.make_async_copy(act, act_hbm, out_sem.at[0]),
         pltpu.make_async_copy(dh, dh_hbm, out_sem.at[1]),
     ]
     start_all(last)
-    wait_all(stores)
+    for k in range(STEPS):
+        wait_all(stores(k))
     wait_all(last)
 
 
 def layer_second(
-    half_ref, n_hbm, cott_hbm, up_hbm, down_hbm, act_hbm, dh_hbm, g_hbm, *refs
+    half_ref, rank_ref, n_hbm, cott_hbm, up_hbm, down_hbm, act_hbm, dh_hbm, g_hbm, cross, keep, *refs
 ):
-    sends = refs[:MP]
-    n, nt, cott, up, down, act, dh, g, in_sem, w_sem, g_sem = refs[MP : MP + 11]
-    up_o, down_o, act_o, dh_o, dn, packed, wo_sem = refs[MP + 11 :]
+    n, nt, cott, cot, up, down, act, dh, g, in_sem, w_sem, g_sem = refs[:12]
+    up_o, down_o, act_o, dh_o, dn, packed, wo_sem = refs[12:]
     first = [
         pltpu.make_async_copy(n_hbm, n, in_sem.at[0]),
         pltpu.make_async_copy(cott_hbm, cott, in_sem.at[1]),
     ]
     half = half_ref[0]
-    loads = weight_loads(half, up_hbm, down_hbm, up, down, w_sem)
-    others = weight_loads(1 - half, up_hbm, down_hbm, up_o, down_o, wo_sem)
+    loads = lambda k: weight_loads(half, up_hbm, down_hbm, up, down, w_sem, k)
+    stores = lambda k: gradient_stores(g, g_hbm, g_sem, k)
     late = [
         pltpu.make_async_copy(act_hbm, act_o, in_sem.at[2]),
         pltpu.make_async_copy(dh_hbm, dh_o, in_sem.at[3]),
     ]
-    for pair in others:
-        late += pair
+    for k in range(STEPS):
+        late += weight_loads(1 - half, up_hbm, down_hbm, up_o, down_o, wo_sem, k)
     start_all(first)
-    for pair in loads:
-        start_all(pair)
+    for k in range(STEPS):
+        start_all(loads(k))
     start_all(late)
     wait_all(first)
-    rows = n[...]
-    nt[...] = rows.T
-    cot = cott[...].T
-    stores = layer_half(loads, rows, nt[...], cot, up, down, act, dh, g, g_hbm, g_sem)
+    nt[...] = n[...].T
+    cot[...] = cott[...].T
+    layer_half(loads, stores, n, nt, cot, up, down, act, dh, g)
     wait_all(late)
     out = dot(act[...], down[...]) + dot(act_o[...], down_o[...])
     out = out.T
@@ -304,14 +323,16 @@
             at = p * 64 + a * 16
             packed[p, :, a * U : (a + 1) * U] = out[at : at + 16, :].astype(bf16)
     dn[...] = dot(dh[...], up[...], NT) + dot(dh_o[...], up_o[...], NT)
-    for s in range(MP):
-        p = half_ref[1] ^ s
-        sends[s][0:UB, :] = dn[pl.ds(pl.multiple_of(p * UB, UB), UB), :].astype(bf16)
-        sends[s][UB:, :] = packed[p]
-    wait_all(stores)
-
-
-def layer_call(half, n, cott, up, down, others=()):
+    for k in range(4):
+        for flip, to in ((1, cross), (0, keep)):
+            p = rank_ref[0] ^ flip ^ (2 * k)
+            to[k, 0:UB, :] = dn[pl.ds(pl.multiple_of(p * UB, UB), UB), :].astype(bf16)
+            to[k, UB:, :] = packed[p]
+    for k in range(STEPS):
+        wait_all(stores(k))
+
+
+def layer_call(half, rank, n, cott, up, down, others=()):
     wide, tall = pltpu.VMEM((E * R, HALF), bf16), pltpu.VMEM((HALF, 512), bf16)
     slab = pltpu.VMEM((U, HALF), bf16)
     sems = lambda *shape: pltpu.SemaphoreType.DMA(shape)
@@ -319,6 +340,7 @@
         pltpu.VMEM((U, E * R), bf16),
         pltpu.VMEM((E * R, U), bf16),
         pltpu.VMEM((512, U), bf16),
+        pltpu.VMEM((U, 512), bf16),
         wide, tall, slab, slab,
         pltpu.VMEM((MP, 192, 1024), bf16),
     ]
@@ -328,8 +350,8 @@
         scratch += [sems(4), sems(2, STEPS), sems(2, STEPS)]
         scratch += [wide, tall, slab, slab, pltpu.VMEM((U, E * R), f32)]
         scratch += [pltpu.VMEM((MP, 16, 1024), bf16), sems(2, STEPS)]
-        out_specs = [HBM] + [VMEM] * MP
-        out_shape = [g_shape] + [jax.ShapeDtypeStruct((48, 1024), bf16)] * MP
+        out_specs = [HBM] + [VMEM] * 2
+        out_shape = [g_shape] + [jax.ShapeDtypeStruct((4, 48, 1024), bf16)] * 2
     else:
         body = layer_first
         scratch += [sems(2), sems(2, STEPS), sems(2, STEPS), sems(2)]
@@ -337,26 +359,47 @@
         out_shape = [g_shape] + [jax.ShapeDtypeStruct((U, HALF), bf16)] * 2
     return pl.pallas_call(
         body,
-        in_specs=[pl.BlockSpec(memory_space=pltpu.SMEM)] + [HBM] * (4 + len(others)),
+        in_specs=[pl.BlockSpec(memory_space=pltpu.SMEM)] * 2 + [HBM] * (4 + len(others)),
         out_specs=out_specs,
         out_shape=out_shape,
         scratch_shapes=scratch,
         name="layer_second" if others else "layer_first",
-    )(half, n, cott, up, down, *others)
+    )(half, rank, n, cott, up, down, *others)
+
+
+def pair_kernel(own, got, out_hbm, total, sem):
+    stores = [pltpu.make_async_copy(total.at[t], out_hbm.at[t], sem.at[t]) for t in range(8)]
+    for t in range(8):
+        total[t] = (own[t].astype(f32) + got[t].astype(f32)).astype(bf16)
+        stores[t].start()
+    wait_all(stores)
+
+
+def pair_call(own, got):
+    shape = (8, 192, 1024)
+    return pl.pallas_call(
+        pair_kernel,
+        in_specs=[VMEM, VMEM],
+        out_specs=HBM,
+        out_shape=jax.ShapeDtypeStruct(shape, bf16),
+        scratch_shapes=[pltpu.VMEM(shape, bf16), pltpu.SemaphoreType.DMA((8,))],
+        compiler_params=pltpu.CompilerParams(vmem_limit_bytes=24 * 2**20),
+        name="pair_sum",
+    )(own, got)
 
 
 def fm_back_kernel(rank_ref, *refs):
-    dns = refs[:MP]
-    recv_ref, projpad_ref, normed_ref, inv_ref, mix_ref = refs[MP : MP + 5]
-    sends = refs[MP + 5 : 2 * MP + 5]
-    block_ref, scr, rows = refs[2 * MP + 5 :]
+    dns = refs[:4]
+    recv_ref, projpad_ref, normed_ref, inv_ref, mix_ref = refs[4:9]
+    sends = refs[9 : 9 + MP]
+    block_ref, scr, rows = refs[9 + MP :]
     mask = flat_mask()
     inv = inv_ref[...][:, 0:1]
     dots = jnp.zeros((UB, 1), f32)
     for j in range(MP):
         at = slice(j * E, (j + 1) * E)
         d = dns[0][0:UB, at].astype(f32)
-        for s in range(1, MP):
+        for s in range(1, 4):
             d = d + dns[s][0:UB, at].astype(f32)
         scr[pl.ds(j, UB, stride=R), :] = d
         dots = dots + jnp.sum(d * normed_ref[:, at], axis=1, keepdims=True)
@@ -386,11 +429,11 @@
             rows[j, pl.ds(pl.multiple_of(u * FH, FH), FH), :] = grad[j * FH : (j + 1) * FH, :]
         return carry
 
-    lax.fori_loop(0, UB, step, 0, unroll=16)
+    lax.fori_loop(0, UB, step, 0, unroll=32)
     for s in range(MP):
         sends[s][...] = rows[rank_ref[0] ^ s]
     out = dns[0][UB : UB + 16, :].astype(f32)
-    for s in range(1, MP):
+    for s in range(1, 4):
         out = out + dns[s][UB : UB + 16, :].astype(f32)
     out = out.astype(bf16)
     for a in range(4):
@@ -478,16 +521,11 @@
 HALVES = [jax.ShapeDtypeStruct((1024, 2048), f32), jax.ShapeDtypeStruct((2048, 512), f32)]
 
 
-def half_kernel(half_ref, stack_hbm, *refs):
-    up_hbm, down_hbm, stack, up, down, in_sem, up_sem, down_sem = refs[-8:]
-    loads = [
-        pltpu.make_async_copy(stack_hbm.at[i], stack.at[i], in_sem.at[i]) for i in range(8)
-    ]
-    start_all(loads)
+def half_kernel(half_ref, stack, *refs):
+    up_hbm, down_hbm, up, down, up_sem, down_sem = refs[-6:]
     cols = pl.ds(pl.multiple_of(half_ref[0] * HALF, HALF), HALF)
     stores = []
     for i in range(8):
-        loads[i].wait()
         at = i * E
         up[at : at + E, :] = stack[i, 0:E, :].astype(f32)
         down[at : at + 64, :] = stack[i, E:, 0:512].astype(f32)
@@ -505,16 +543,13 @@
 def half_call(half, stack, outs=()):
     return pl.pallas_call(
         half_kernel,
-        in_specs=[pl.BlockSpec(memory_space=pltpu.SMEM)] + [HBM] * (1 + len(outs)),
+        in_specs=[pl.BlockSpec(memory_space=pltpu.SMEM), VMEM] + [HBM] * len(outs),
         out_specs=[HBM, HBM],
         out_shape=HALVES,
-        scratch_shapes=[
-            pltpu.VMEM((8,) + CHUNK, bf16),
-            pltpu.VMEM((1024, 1024), f32),
-            pltpu.VMEM((1024, 512), f32),
-        ]
-        + [pltpu.SemaphoreType.DMA((8,))] * 3,
+        scratch_shapes=[pltpu.VMEM((1024, 1024), f32), pltpu.VMEM((1024, 512), f32)]
+        + [pltpu.SemaphoreType.DMA((8,))] * 2,
         input_output_aliases={2: 0, 3: 1} if outs else {},
+        compiler_params=pltpu.CompilerParams(vmem_limit_bytes=24 * 2**20),
         name="other_half" if outs else "own_half",
     )(half, stack, *outs)
 
@@ -528,12 +563,16 @@
 
 def core_swap(x):
     return lax.ppermute(x, "dp", [(i, i ^ 1) for i in range(16)])
+
+
+def mp_permute(x, s):
+    return lax.ppermute(x, "mp", [(i, i ^ s) for i in range(MP)])
 
 
 def exchange_slots(xs):
     got = [xs[0]]
     for s in range(1, MP):
-        got.append(lax.ppermute(xs[s], "mp", [(i, i ^ s) for i in range(MP)]))
+        got.append(mp_permute(xs[s], s))
     return got
 
 
@@ -566,14 +605,16 @@
     mine = c[None].astype(jnp.int32)
     rank = m[None].astype(jnp.int32)
     slots = (m ^ jnp.arange(MP)).astype(jnp.int32)
-    layer = (n, cot_full, up_weight, down_weight)
+    layer = (rank, n, cot_full, up_weight, down_weight)
     g_other, *others = layer_call(other, *layer)
     got = core_swap(g_other)
-    g_mine, *dn_sends = layer_call(jnp.concatenate([mine, rank]), *layer, tuple(others))
-    pair = (g_mine.astype(f32) + got.astype(f32)).astype(bf16)
+    g_mine, cross, keep = layer_call(mine, *layer, tuple(others))
+    crossed = mp_permute(cross, 1)
+    pair = pair_call(g_mine, got)
     parts = dp_exchange(pair)
 
-    dns = exchange_slots(dn_sends)
+    dns = [(keep[k].astype(f32) + crossed[k].astype(f32)).astype(bf16) for k in range(4)]
+    dns = dns[:1] + [mp_permute(dns[k], 2 * k) for k in range(1, 4)]
     *gp_sends, block_out = fm_back_call(rank, dns, recv, projpad, normed, inv, mix)
 
     chunk = jnp.sum(parts.astype(f32), axis=0).astype(bf16)

time: 253 us -> 253 us (level)
  waiting for transfers between devices: 45.5 us -> 55.5 us
  starting transfers between devices: 47.1 us -> 37.5 us
  other arithmetic: 6.43 us -> 3.25 us
    ppermute x14 -> x11, waiting for transfers between devices: 12.9 us -> 22.8 us  [mp_permute(): return lax.ppermute(x, 'mp', [(i, i ^ s) for i in range(MP)])]
    ppermute x14 -> x11, starting transfers between devices: 24.9 us -> 15.6 us  [mp_permute(): return lax.ppermute(x, 'mp', [(i, i ^ s) for i in range(MP)])]
    convert_element_type x1, other arithmetic: 3.44 us -> 0.8 us  [device_step(): (keep[k].astype(f32) + crossed[k].astype(f32)).astype(bf16)]
    pallas_call x3 -> x4, Pallas kernels: 22.7 us -> 24.3 us  [the longest x2 16.6 us: layer_call(): pl.pallas_call(body, in_specs=[pl.BlockSpec(memory_space=pltpu.SMEM)] * 2...]
  transfers between devices with their start and end apart: 26 -> 23, of which waited for: 13 -> 14; matrix products, arithmetic and copies ran while one was open for 1% -> 2% of each run, Pallas kernels for 13% -> 12%
where the time goes in v3:
time: 253 us; the launch traced here: 252 us
  blocking collectives  90.1 us (36%)
  Pallas kernels  59 us (23%)
  waiting for transfers between devices  55.5 us (22%)
  starting transfers between devices  37.5 us (15%)
  local copies, waits for them, and re-layouts  6.14 us (2%)
  other arithmetic  3.25 us (1%)
    all_to_all x2, blocking collectives, dp_exchange(): lax.all_to_all(x, 'dp', 0, 0, axis_index_groups=SAME_CORE, tiled=True)  90.1 us
    all_to_all x2, waiting for transfers between devices, exchange(): return lax.all_to_all(x, 'mp', 0, 0, tiled=True)  27.4 us
    ppermute x11, waiting for transfers between devices, mp_permute(): return lax.ppermute(x, 'mp', [(i, i ^ s) for i in range(MP)])  22.8 us
    pallas_call x2, Pallas kernels, layer_call(): pl.pallas_call(body, in_specs=[pl.BlockSpec(memory_space=pltpu.SMEM)] * 2...  16.6 us
    ppermute x11, starting transfers between devices, mp_permute(): return lax.ppermute(x, 'mp', [(i, i ^ s) for i in range(MP)])  15.6 us
    ppermute x7, starting transfers between devices, dp_permute(): return lax.ppermute(x, 'dp', pairs)  12.8 us
    pallas_call x1, Pallas kernels, query_call(): pl.pallas_call(query_kernel, grid_spec=pltpu.PrefetchScalarGridSpec(num_s...  12.2 us
    all_to_all x2, starting transfers between devices, exchange(): return lax.all_to_all(x, 'mp', 0, 0, tiled=True)  9.03 us
  transfers between devices with their start and end apart: 23, of which 14 were waited for; matrix products, arithmetic and copies ran while one was open for 2% of the time, Pallas kernels for 12%

profile of v3, /device:TPU:0, one launch (start us, length us, event | category | flops | bytes accessed | tf_op | source)
XLA Modules:
  0.0 252.5 jit_solution(14303172634033620048)
XLA Ops:
  0.6 9.0 %pool.1 = (bf16[8,640,128]{2,1,0:T(8,128)(2,1)}, f32[256,128]{1,0:T(8,128)}) custom-call(bf16[32768,128]{1,0:T(8,128)(2,1)} %bitcast.18, s32[16,256]{1,0:T(8,128)} %bitcast.23, bf16[16,128]{1,0:T(8,128)(2,1)} %q_ref.1, bf16[64,256]{1,0:T(8,128)(2,1)} %bitcast.22), custom_call_target="tpu_custom_call" | custom-call | tf_op jit(solution)/shard_map/pool/pallas_call | solution.py:104
  9.6 5.5 %all-to-all-start = ((bf16[8,640,128]{2,1,0:T(8,128)(2,1)}), bf16[8,640,128]{2,1,0:T(8,128)(2,1)S(1)}, u32[]{:S(2)}, u32[]{:S(2)}) async-start(bf16[8,640,128]{2,1,0:T(8,128)(2,1)} %get-tuple-element.33), calls=%async_computation | async-start | bytes 2621440 | tf_op jit(solution)/shard_map/all_to_all | solution.py:590
  15.1 0.6 pad.8.projt_ref
  15.7 17.9 %all-to-all-done.recv_ref.refs_4_ = bf16[8,640,128]{2,1,0:T(8,128)(2,1)S(1)} async-done(((bf16[8,640,128]{2,1,0:T(8,128)(2,1)}), bf16[8,640,128]{2,1,0:T(8,128)(2,1)S(1)}, u32[]{:S(2)}, u32[]{:S(2)}) %all-to-all-start) | async-done | bytes 1310752 | tf_op jit(solution)/shard_map/all_to_all | solution.py:590
  33.7 1.1 copy-done.1
  34.8 5.4 %fm_forward.1 = (bf16[8,32,1024]{2,1,0:T(8,128)(2,1)}, f32[32,1024]{1,0:T(8,128)}, f32[32,128]{1,0:T(8,128)}, f32[256,128]{1,0:T(8,128)}, bf16[512,256]{1,0:T(8,128)(2,1)}) custom-call(bf16[8,640,128]{2,1,0:T(8,128)(2,1)} %copy-done.1, bf16[16,128]{1,0:T(8,128)(2,1)} %pad.8.projt_ref), custom_call_target="tpu_custom_call" | custom-call | tf_op jit(solution)/shard_map/fm_forward/pallas_call | solution.py:181
  40.2 3.5 %all-to-all-start.1 = ((bf16[8,32,1024]{2,1,0:T(8,128)(2,1)}), bf16[8,32,1024]{2,1,0:T(8,128)(2,1)S(1)}, u32[]{:S(2)}, u32[]{:S(2)}) async-start(bf16[8,32,1024]{2,1,0:T(8,128)(2,1)} %get-tuple-element.34), calls=%async_computation.1 | async-start | bytes 1048576 | tf_op jit(solution)/shard_map/all_to_all | solution.py:590
  43.7 9.4 %all-to-all-done.1 = bf16[8,32,1024]{2,1,0:T(8,128)(2,1)S(1)} async-done(((bf16[8,32,1024]{2,1,0:T(8,128)(2,1)}), bf16[8,32,1024]{2,1,0:T(8,128)(2,1)S(1)}, u32[]{:S(2)}, u32[]{:S(2)}) %all-to-all-start.1) | async-done | bytes 524320 | tf_op jit(solution)/shard_map/all_to_all | solution.py:590
  53.2 0.8 copy-done.2
  53.9 7.3 %layer_first.1 = (bf16[8,192,1024]{2,1,0:T(8,128)(2,1)}, bf16[256,1024]{1,0:T(8,128)(2,1)}, bf16[256,1024]{1,0:T(8,128)(2,1)}) custom-call(s32[1]{0:T(128)} %bitcast.7.half_ref, s32[1]{0:T(128)} %bitcast.rank_ref, bf16[256,1024]{1,0:T(8,128)(2,1)} %bitcast.20, bf16[512,256]{1,0:T(8,128)(2,1)} %get-tuple-element.35.cott_hbm, bf16[1024,2048]{1,0:T(8,128)(2,1)} %up_hbm.3, ...), custom_call_target="tpu_custom_call" | custom-call | tf_op jit(solution)/shard_map/layer_first/pallas_call | solution.py:360
  61.2 0.1 collective-permute-start.4
  61.3 9.3 %layer_second.1 = (bf16[8,192,1024]{2,1,0:T(8,128)(2,1)}, bf16[4,48,1024]{2,1,0:T(8,128)(2,1)}, bf16[4,48,1024]{2,1,0:T(8,128)(2,1)}) custom-call(s32[1]{0:T(128)} %bitcast.1.half_ref, s32[1]{0:T(128)} %bitcast.rank_ref, bf16[256,1024]{1,0:T(8,128)(2,1)} %bitcast.21, bf16[512,256]{1,0:T(8,128)(2,1)} %get-tuple-element.35.cott_hbm, ...), custom_call_target="tpu_custom_call" | custom-call | tf_op jit(solution)/shard_map/layer_second/pallas_call | solution.py:360
  70.6 0.0 collective-permute-done.4.got
  70.6 0.0 copy-start
  70.6 1.9 copy-done
  72.5 2.3 pair_sum.1
  74.8 47.4 %all_to_all.20 = bf16[8,192,1024]{2,1,0:T(8,128)(2,1)S(1)} all-to-all(bf16[8,192,1024]{2,1,0:T(8,128)(2,1)S(1)} %pair_sum.1), channel_id=1, replica_groups={{0,16,32,48,64,80,96,112},{8,24,40,56,72,88,104,120},{1,17,33,49,65,81,..., dimensions={0} | all-to-all | bytes 6291456 | tf_op jit(solution)/shard_map/all_to_all | solution.py:561
  122.3 0.6 reduce_sum.12
  122.9 0.4 broadcast_in_dim.18
  123.3 42.7 %all_to_all.21.stack = bf16[8,192,1024]{2,1,0:T(8,128)(2,1)S(1)} all-to-all(bf16[8,192,1024]{2,1,0:T(8,128)(2,1)S(1)} %broadcast_in_dim.18), channel_id=1, replica_groups={{0,16,32,48,64,80,96,112},{8,24,40,56,72,88,104,120},{1,17,33,49,65,81,..., dimensions={0} | all-to-all | bytes 6291456 | tf_op jit(solution)/shard_map/all_to_all | solution.py:561
  166.0 0.7 collective-permute-start
  166.6 10.9 %collective-permute-done = bf16[4,48,1024]{2,1,0:T(8,128)(2,1)S(1)} collective-permute-done((bf16[4,48,1024]{2,1,0:T(8,128)(2,1)S(1)}, bf16[4,48,1024]{2,1,0:T(8,128)(2,1)S(1)}, u32[]{:S(2)}, u32[]{:S(2)}) %collective-permute-start) | collective-permute-done | bytes 393248 | tf_op jit(solution)/shard_map/ppermute | solution.py:569
  177.5 0.8 fusion.3
  178.3 0.9 collective-permute-start.3
  179.2 1.4 collective-permute-start.2
  180.5 1.9 collective-permute-start.1
  182.4 0.1 copy.16
  182.5 0.6 pad.9.refs_5_
  183.2 3.0 %collective-permute-done.3.refs_3_ = bf16[48,1024]{1,0:T(8,128)(2,1)S(1)} collective-permute-done((bf16[48,1024]{1,0:T(8,128)(2,1)}, bf16[48,1024]{1,0:T(8,128)(2,1)S(1)}, u32[]{:S(2)}, u32[]{:S(2)}) %collective-permute-start.3) | collective-permute-done | bytes 98336 | tf_op jit(solution)/shard_map/ppermute | solution.py:569
  186.2 0.6 collective-permute-done.1.refs_1_
  186.8 0.1 copy-done.7
  186.8 0.0 copy-done.8
  186.9 0.5 copy-done.9
  187.4 6.1 %fm_backward.1 = (bf16[512,128]{1,0:T(8,128)(2,1)}, bf16[512,128]{1,0:T(8,128)(2,1)}, bf16[512,128]{1,0:T(8,128)(2,1)}, bf16[512,128]{1,0:T(8,128)(2,1)}, bf16[5...) custom-call(s32[1]{0:T(128)} %bitcast.rank_ref, ...), custom_call_target="tpu_custom_call" | custom-call | tf_op jit(solution)/shard_map/fm_backward/pallas_call | solution.py:446
  193.5 0.7 collective-permute-start.6
  194.2 0.7 collective-permute-start.7
  194.8 2.1 collective-permute-start.8
  197.0 1.2 collective-permute-start.9
  198.2 1.1 collective-permute-done.6.refs_1_
  199.3 1.9 collective-permute-start.10
  201.1 2.6 %collective-permute-done.7.refs_2_ = bf16[512,128]{1,0:T(8,128)(2,1)S(1)} collective-permute-done((bf16[512,128]{1,0:T(8,128)(2,1)}, bf16[512,128]{1,0:T(8,128)(2,1)S(1)}, u32[]{:S(2)}, u32[]{:S(2)}) %collective-permute-start.7) | collective-permute-done | bytes 131104 | tf_op jit(solution)/shard_map/ppermute | solution.py:569
  203.7 2.0 collective-permute-start.11
  205.8 2.2 collective-permute-start.12
  208.0 0.5 iota_xor_fusion.idx_ref
  208.5 0.3 collective-permute-done.9.refs_4_
  208.9 2.1 collective-permute-done.11.refs_6_
  211.0 2.2 collective-permute-done.12.refs_7_
  213.2 12.2 %query_gradient.1 = (f32[16,128]{1,0:T(8,128)}, bf16[4096,128]{1,0:T(8,128)(2,1)}) custom-call(s32[8]{0:T(128)} %iota_xor_fusion.idx_ref, bf16[32768,128]{1,0:T(8,128)(2,1)} %bitcast.19, bf16[512,128]{1,0:T(8,128)(2,1)} %get-tuple-element.50.refs_0_, bf16[512,128]{1,0:T(8,128)(2,1)} %copy-done.4, bf16[512,128]{1,0:T(8,128)(2,1)} %copy-done.5, ...), custom_call_target="tpu_custom_call" | custom-call | tf_op jit(solution)/shard_map/query_gradient/pallas_call | solution.py:498
  225.4 0.0 collective-permute-start.13
  225.4 1.4 collective-permute-done.13
  226.8 0.7 add_convert_fusion.4
  227.5 1.7 collective-permute-start.20
  229.2 3.0 %collective-permute-start.19 = (bf16[16,128]{1,0:T(8,128)(2,1)S(1)}, bf16[16,128]{1,0:T(8,128)(2,1)S(1)}, u32[]{:S(2)}, u32[]{:S(2)}) collective-permute-start(bf16[16,128]{1,0:T(8,128)(2,1)S(1)} %add_convert_fusion.4), channel_id=1, source_target_pairs={{0,96},{8,104},{16,112},{24,120},{32,64},{40,72},{48,80},{56,88},{... | collective-permute-start | bytes 12296 | tf_op jit(solution)/shard_map/ppermute | solution.py:586
  232.1 0.5 collective-permute-start.18
  232.7 2.5 collective-permute-start.17
  235.2 3.2 %collective-permute-start.16 = (bf16[16,128]{1,0:T(8,128)(2,1)S(1)}, bf16[16,128]{1,0:T(8,128)(2,1)S(1)}, u32[]{:S(2)}, u32[]{:S(2)}) collective-permute-start(bf16[16,128]{1,0:T(8,128)(2,1)S(1)} %add_convert_fusion.4), channel_id=1, source_target_pairs={{0,48},{8,56},{16,0},{24,8},{32,16},{40,24},{48,32},{56,40},{64,11... | collective-permute-start | bytes 12296 | tf_op jit(solution)/shard_map/ppermute | solution.py:586
  238.4 0.9 collective-permute-start.15
  239.2 0.2 collective-permute-done.18
  239.4 1.1 collective-permute-start.14
  240.4 3.0 %collective-permute-done.15 = bf16[16,128]{1,0:T(8,128)(2,1)S(1)} collective-permute-done((bf16[16,128]{1,0:T(8,128)(2,1)S(1)}, bf16[16,128]{1,0:T(8,128)(2,1)S(1)}, u32[]{:S(2)}, u32[]{:S(2)}) %collective-permute-start.15) | collective-permute-done | bytes 4128 | tf_op jit(solution)/shard_map/ppermute | solution.py:586
  243.5 0.7 collective-permute-done.14
  244.2 0.6 convert_add_fusion
  244.8 2.8 %own_half.1 = (f32[1024,2048]{1,0:T(8,128)}, f32[2048,512]{1,0:T(8,128)}) custom-call(s32[1]{0:T(128)} %bitcast.1.half_ref, bf16[8,192,1024]{2,1,0:T(8,128)(2,1)S(1)} %all_to_all.21.stack), custom_call_target="tpu_custom_call" | custom-call | tf_op jit(solution)/shard_map/own_half/pallas_call | solution.py:544
  247.6 4.7 %other_half.1 = (f32[1024,2048]{1,0:T(8,128)}, f32[2048,512]{1,0:T(8,128)}) custom-call(s32[1]{0:T(128)} %bitcast.7.half_ref, bf16[8,192,1024]{2,1,0:T(8,128)(2,1)} %collective-permute-done.5.stack, f32[1024,2048]{1,0:T(8,128)} %get-tuple-element.46.refs_0_, f32[2048,512]{1,0:T(8,128)} %get-tuple-element.47.refs_1_), custom_call_target="tpu_custom_call", output_to_operand_aliasing={{0}: (2, {}), {1}: (3, {})} | custom-call | tf_op jit(solution)/shard_map/other_half/pallas_call | solution.py:544
  (27 shorter events, 0.1 us)
Async XLA Ops:
  0.6 14.5 %copy-start.10 = (bf16[128,8]{0,1:T(8,128)(2,1)S(1)}, bf16[128,8]{0,1:T(8,128)(2,1)}, u32[]{:S(2)}) copy-start(bf16[128,8]{0,1:T(8,128)(2,1)} %param.10) | copy-start | bytes 6148
  9.6 24.1 %all-to-all-start = ((bf16[8,640,128]{2,1,0:T(8,128)(2,1)}), bf16[8,640,128]{2,1,0:T(8,128)(2,1)S(1)}, u32[]{:S(2)}, u32[]{:S(2)}) async-start(bf16[8,640,128]{2,1,0:T(8,128)(2,1)} %get-tuple-element.33), calls=%async_computation | async-start | bytes 2621440 | tf_op jit(solution)/shard_map/all_to_all | solution.py:590
  33.7 1.1 copy-start.1
  40.2 13.0 %all-to-all-start.1 = ((bf16[8,32,1024]{2,1,0:T(8,128)(2,1)}), bf16[8,32,1024]{2,1,0:T(8,128)(2,1)S(1)}, u32[]{:S(2)}, u32[]{:S(2)}) async-start(bf16[8,32,1024]{2,1,0:T(8,128)(2,1)} %get-tuple-element.34), calls=%async_computation.1 | async-start | bytes 1048576 | tf_op jit(solution)/shard_map/all_to_all | solution.py:590
  53.1 0.8 copy-start.2
  61.2 9.4 %collective-permute-start.4 = (bf16[8,192,1024]{2,1,0:T(8,128)(2,1)}, bf16[8,192,1024]{2,1,0:T(8,128)(2,1)S(1)}, u32[]{:S(2)}, u32[]{:S(2)}) collective-permute-start(bf16[8,192,1024]{2,1,0:T(8,128)(2,1)} %get-tuple-element.45), channel_id=1, source_target_pairs={{0,8},{8,0},{16,24},{24,16},{32,40},{40,32},{48,56},{56,48},{64,72... | collective-permute-start | bytes 9437192 | tf_op jit(solution)/shard_map/ppermute | solution.py:565
  70.6 1.9 copy-start
  123.3 42.7 %copy-start.11 = (bf16[4,48,1024]{2,1,0:T(8,128)(2,1)S(1)}, bf16[4,48,1024]{2,1,0:T(8,128)(2,1)}, u32[]{:S(2)}) copy-start(bf16[4,48,1024]{2,1,0:T(8,128)(2,1)} %get-tuple-element.39) | copy-start | bytes 1179652
  123.3 54.2 %copy-start.3 = (bf16[4,48,1024]{2,1,0:T(8,128)(2,1)S(1)}, bf16[4,48,1024]{2,1,0:T(8,128)(2,1)}, u32[]{:S(2)}) copy-start(bf16[4,48,1024]{2,1,0:T(8,128)(2,1)} %get-tuple-element.38) | copy-start | bytes 1179652
  166.0 81.6 %collective-permute-start.5 = (bf16[8,192,1024]{2,1,0:T(8,128)(2,1)S(1)}, bf16[8,192,1024]{2,1,0:T(8,128)(2,1)}, u32[]{:S(2)}, u32[]{:S(2)}) collective-permute-start(bf16[8,192,1024]{2,1,0:T(8,128)(2,1)S(1)} %all_to_all.21.stack), channel_id=1, source_target_pairs={{0,8},{8,0},{16,24},{24,16},{32,40},{40,32},{48,56},{56,48},{64,72... | collective-permute-start | bytes 9437192 | tf_op jit(solution)/shard_map/ppermute | solution.py:565
  166.0 11.5 %collective-permute-start = (bf16[4,48,1024]{2,1,0:T(8,128)(2,1)S(1)}, bf16[4,48,1024]{2,1,0:T(8,128)(2,1)S(1)}, u32[]{:S(2)}, u32[]{:S(2)}) collective-permute-start(bf16[4,48,1024]{2,1,0:T(8,128)(2,1)S(1)} %copy-done.11), channel_id=1, source_target_pairs={{0,1},{1,0},{2,3},{3,2},{4,5},{5,4},{6,7},{7,6},{8,9},{9,8},{10,11... | collective-permute-start | bytes 1179656 | tf_op jit(solution)/shard_map/ppermute | solution.py:569
  178.3 7.9 %collective-permute-start.3 = (bf16[48,1024]{1,0:T(8,128)(2,1)}, bf16[48,1024]{1,0:T(8,128)(2,1)S(1)}, u32[]{:S(2)}, u32[]{:S(2)}) collective-permute-start(bf16[48,1024]{1,0:T(8,128)(2,1)} %get-tuple-element.61), channel_id=1, source_target_pairs={{0,6},{1,7},{2,4},{3,5},{4,2},{5,3},{6,0},{7,1},{8,14},{9,15},{10,... | collective-permute-start | bytes 294920 | tf_op jit(solution)/shard_map/ppermute | solution.py:569
  179.2 7.0 %collective-permute-start.2 = (bf16[48,1024]{1,0:T(8,128)(2,1)}, bf16[48,1024]{1,0:T(8,128)(2,1)S(1)}, u32[]{:S(2)}, u32[]{:S(2)}) collective-permute-start(bf16[48,1024]{1,0:T(8,128)(2,1)} %get-tuple-element.62), channel_id=1, source_target_pairs={{0,4},{1,5},{2,6},{3,7},{4,0},{5,1},{6,2},{7,3},{8,12},{9,13},{10,... | collective-permute-start | bytes 294920 | tf_op jit(solution)/shard_map/ppermute | solution.py:569
  180.5 6.2 %collective-permute-start.1 = (bf16[48,1024]{1,0:T(8,128)(2,1)}, bf16[48,1024]{1,0:T(8,128)(2,1)S(1)}, u32[]{:S(2)}, u32[]{:S(2)}) collective-permute-start(bf16[48,1024]{1,0:T(8,128)(2,1)} %get-tuple-element.63), channel_id=1, source_target_pairs={{0,2},{1,3},{2,0},{3,1},{4,6},{5,7},{6,4},{7,5},{8,10},{9,11},{10,... | collective-permute-start | bytes 294920 | tf_op jit(solution)/shard_map/ppermute | solution.py:569
  186.2 0.6 copy-start.7
  186.2 0.7 copy-start.8
  186.8 0.6 copy-start.9
  193.5 5.8 %collective-permute-start.6 = (bf16[512,128]{1,0:T(8,128)(2,1)}, bf16[512,128]{1,0:T(8,128)(2,1)S(1)}, u32[]{:S(2)}, u32[]{:S(2)}) collective-permute-start(bf16[512,128]{1,0:T(8,128)(2,1)} %get-tuple-element.51), channel_id=1, source_target_pairs={{0,1},{1,0},{2,3},{3,2},{4,5},{5,4},{6,7},{7,6},{8,9},{9,8},{10,11... | collective-permute-start | bytes 393224 | tf_op jit(solution)/shard_map/ppermute | solution.py:569
  194.2 9.6 %collective-permute-start.7 = (bf16[512,128]{1,0:T(8,128)(2,1)}, bf16[512,128]{1,0:T(8,128)(2,1)S(1)}, u32[]{:S(2)}, u32[]{:S(2)}) collective-permute-start(bf16[512,128]{1,0:T(8,128)(2,1)} %get-tuple-element.52), channel_id=1, source_target_pairs={{0,2},{1,3},{2,0},{3,1},{4,6},{5,7},{6,4},{7,5},{8,10},{9,11},{10,... | collective-permute-start | bytes 393224 | tf_op jit(solution)/shard_map/ppermute | solution.py:569
  194.8 10.9 %collective-permute-start.8 = (bf16[512,128]{1,0:T(8,128)(2,1)}, bf16[512,128]{1,0:T(8,128)(2,1)S(1)}, u32[]{:S(2)}, u32[]{:S(2)}) collective-permute-start(bf16[512,128]{1,0:T(8,128)(2,1)} %get-tuple-element.53), channel_id=1, source_target_pairs={{0,3},{1,2},{2,1},{3,0},{4,7},{5,6},{6,5},{7,4},{8,11},{9,10},{10,... | collective-permute-start | bytes 393224 | tf_op jit(solution)/shard_map/ppermute | solution.py:569
  197.0 11.9 %collective-permute-start.9 = (bf16[512,128]{1,0:T(8,128)(2,1)}, bf16[512,128]{1,0:T(8,128)(2,1)}, u32[]{:S(2)}, u32[]{:S(2)}) collective-permute-start(bf16[512,128]{1,0:T(8,128)(2,1)} %get-tuple-element.54), channel_id=1, source_target_pairs={{0,4},{1,5},{2,6},{3,7},{4,0},{5,1},{6,2},{7,3},{8,12},{9,13},{10,... | collective-permute-start | bytes 393224 | tf_op jit(solution)/shard_map/ppermute | solution.py:569
  199.3 13.9 %copy-start.4 = (bf16[512,128]{1,0:T(8,128)(2,1)}, bf16[512,128]{1,0:T(8,128)(2,1)S(1)}, u32[]{:S(2)}) copy-start(bf16[512,128]{1,0:T(8,128)(2,1)S(1)} %collective-permute-done.6.refs_1_) | copy-start | bytes 393220
  199.3 9.6 %collective-permute-start.10 = (bf16[512,128]{1,0:T(8,128)(2,1)}, bf16[512,128]{1,0:T(8,128)(2,1)}, u32[]{:S(2)}, u32[]{:S(2)}) collective-permute-start(bf16[512,128]{1,0:T(8,128)(2,1)} %get-tuple-element.55), channel_id=1, source_target_pairs={{0,5},{1,4},{2,7},{3,6},{4,1},{5,0},{6,3},{7,2},{8,13},{9,12},{10,... | collective-permute-start | bytes 393224 | tf_op jit(solution)/shard_map/ppermute | solution.py:569
  203.7 9.4 %copy-start.5 = (bf16[512,128]{1,0:T(8,128)(2,1)}, bf16[512,128]{1,0:T(8,128)(2,1)S(1)}, u32[]{:S(2)}) copy-start(bf16[512,128]{1,0:T(8,128)(2,1)S(1)} %collective-permute-done.7.refs_2_) | copy-start | bytes 393220
  203.7 7.3 %collective-permute-start.11 = (bf16[512,128]{1,0:T(8,128)(2,1)}, bf16[512,128]{1,0:T(8,128)(2,1)}, u32[]{:S(2)}, u32[]{:S(2)}) collective-permute-start(bf16[512,128]{1,0:T(8,128)(2,1)} %get-tuple-element.56), channel_id=1, source_target_pairs={{0,6},{1,7},{2,4},{3,5},{4,2},{5,3},{6,0},{7,1},{8,14},{9,15},{10,... | collective-permute-start | bytes 393224 | tf_op jit(solution)/shard_map/ppermute | solution.py:569
  205.8 7.4 %copy-start.6 = (bf16[512,128]{1,0:T(8,128)(2,1)}, bf16[512,128]{1,0:T(8,128)(2,1)S(1)}, u32[]{:S(2)}) copy-start(bf16[512,128]{1,0:T(8,128)(2,1)S(1)} %collective-permute-done.8.refs_3_) | copy-start | bytes 393220
  205.8 7.4 %collective-permute-start.12 = (bf16[512,128]{1,0:T(8,128)(2,1)}, bf16[512,128]{1,0:T(8,128)(2,1)}, u32[]{:S(2)}, u32[]{:S(2)}) collective-permute-start(bf16[512,128]{1,0:T(8,128)(2,1)} %get-tuple-element.57), channel_id=1, source_target_pairs={{0,7},{1,6},{2,5},{3,4},{4,3},{5,2},{6,1},{7,0},{8,15},{9,14},{10,... | collective-permute-start | bytes 393224 | tf_op jit(solution)/shard_map/ppermute | solution.py:569
  225.4 1.4 collective-permute-start.13
  227.5 7.7 %collective-permute-start.20 = (bf16[16,128]{1,0:T(8,128)(2,1)S(1)}, bf16[16,128]{1,0:T(8,128)(2,1)S(1)}, u32[]{:S(2)}, u32[]{:S(2)}) collective-permute-start(bf16[16,128]{1,0:T(8,128)(2,1)S(1)} %add_convert_fusion.4), channel_id=1, source_target_pairs={{0,112},{8,120},{16,64},{24,72},{32,80},{40,88},{48,96},{56,104},{... | collective-permute-start | bytes 12296 | tf_op jit(solution)/shard_map/ppermute | solution.py:586
  229.2 9.2 %collective-permute-start.19 = (bf16[16,128]{1,0:T(8,128)(2,1)S(1)}, bf16[16,128]{1,0:T(8,128)(2,1)S(1)}, u32[]{:S(2)}, u32[]{:S(2)}) collective-permute-start(bf16[16,128]{1,0:T(8,128)(2,1)S(1)} %add_convert_fusion.4), channel_id=1, source_target_pairs={{0,96},{8,104},{16,112},{24,120},{32,64},{40,72},{48,80},{56,88},{... | collective-permute-start | bytes 12296 | tf_op jit(solution)/shard_map/ppermute | solution.py:586
  232.1 7.2 %collective-permute-start.18 = (bf16[16,128]{1,0:T(8,128)(2,1)S(1)}, bf16[16,128]{1,0:T(8,128)(2,1)S(1)}, u32[]{:S(2)}, u32[]{:S(2)}) collective-permute-start(bf16[16,128]{1,0:T(8,128)(2,1)S(1)} %add_convert_fusion.4), channel_id=1, source_target_pairs={{0,80},{8,88},{16,96},{24,104},{32,112},{40,120},{48,64},{56,72},{... | collective-permute-start | bytes 12296 | tf_op jit(solution)/shard_map/ppermute | solution.py:586
  232.7 7.8 %collective-permute-start.17 = (bf16[16,128]{1,0:T(8,128)(2,1)S(1)}, bf16[16,128]{1,0:T(8,128)(2,1)S(1)}, u32[]{:S(2)}, u32[]{:S(2)}) collective-permute-start(bf16[16,128]{1,0:T(8,128)(2,1)S(1)} %add_convert_fusion.4), channel_id=1, source_target_pairs={{0,64},{8,72},{16,80},{24,88},{32,96},{40,104},{48,112},{56,120},{... | collective-permute-start | bytes 12296 | tf_op jit(solution)/shard_map/ppermute | solution.py:586
  235.2 5.3 %collective-permute-start.16 = (bf16[16,128]{1,0:T(8,128)(2,1)S(1)}, bf16[16,128]{1,0:T(8,128)(2,1)S(1)}, u32[]{:S(2)}, u32[]{:S(2)}) collective-permute-start(bf16[16,128]{1,0:T(8,128)(2,1)S(1)} %add_convert_fusion.4), channel_id=1, source_target_pairs={{0,48},{8,56},{16,0},{24,8},{32,16},{40,24},{48,32},{56,40},{64,11... | collective-permute-start | bytes 12296 | tf_op jit(solution)/shard_map/ppermute | solution.py:586
  238.4 5.1 %collective-permute-start.15 = (bf16[16,128]{1,0:T(8,128)(2,1)S(1)}, bf16[16,128]{1,0:T(8,128)(2,1)S(1)}, u32[]{:S(2)}, u32[]{:S(2)}) collective-permute-start(bf16[16,128]{1,0:T(8,128)(2,1)S(1)} %add_convert_fusion.4), channel_id=1, source_target_pairs={{0,32},{8,40},{16,48},{24,56},{32,0},{40,8},{48,16},{56,24},{64,96... | collective-permute-start | bytes 12296 | tf_op jit(solution)/shard_map/ppermute | solution.py:586
  239.4 4.8 %collective-permute-start.14 = (bf16[16,128]{1,0:T(8,128)(2,1)S(1)}, bf16[16,128]{1,0:T(8,128)(2,1)S(1)}, u32[]{:S(2)}, u32[]{:S(2)}) collective-permute-start(bf16[16,128]{1,0:T(8,128)(2,1)S(1)} %add_convert_fusion.4), channel_id=1, source_target_pairs={{0,16},{8,24},{16,32},{24,40},{32,48},{40,56},{48,0},{56,8},{64,80... | collective-permute-start | bytes 12296 | tf_op jit(solution)/shard_map/ppermute | solution.py:586
